TPU v7x, 8 devices: a whole 2x2x1 slice. The times are simulated.
8 devices in a mesh: rep: 1 (over z), mp: 2 (over y), tok: 4 (over x, core).
Axes of the slice: x: 2, y: 2, z: 1, core: 2. Of those that a mesh axis runs over, the one named last changes fastest.
Arguments:
- x_in: bfloat16 [2, 512, 5120], P(None, ('rep', 'tok', 'mp'))
- seg_ids: int32 [2, 512], P(None, ('rep', 'tok', 'mp'))
- g_attn: bfloat16 [2, 5120], replicated
- w_q: bfloat16 [2, 5120, 40, 128], P(None, 'tok', 'mp')
- w_k: bfloat16 [2, 5120, 40, 128], P(None, 'tok', 'mp')
- w_v: bfloat16 [2, 5120, 40, 128], P(None, 'tok', 'mp')
- w_o: bfloat16 [2, 40, 128, 5120], P(None, 'mp', None, 'tok')
- g_mlp: bfloat16 [2, 5120], replicated
- w_gate: bfloat16 [2, 5120, 13824], P(None, 'tok', 'mp')
- w_up: bfloat16 [2, 5120, 13824], P(None, 'tok', 'mp')
- w_down: bfloat16 [2, 13824, 5120], P(None, 'mp', 'tok')
Outputs:
- output: float32 [2, 512, 5120], P(None, ('rep', 'tok', 'mp'))
All inputs are finite; a program needn't handle non-finite values.
Results may differ from a plain program's by a relative error of at most 0.0061746.
Values are sent between devices in bfloat16 or wider.
A program may use at most 1 GiB of HBM per device.

v0:
```python
import jax
import jax.numpy as jnp
from jax import lax
from jax.sharding import PartitionSpec as P

NORM_EPS = 1e-5
ROPE_BASE = 10000.0
NEG_BIG = -1e30


def rms_norm(resid, gain_vec):
    mean_sq = jnp.mean(resid * resid, axis=-1, keepdims=True)
    return (resid * lax.rsqrt(mean_sq + NORM_EPS) * gain_vec.astype(jnp.float32)).astype(jnp.bfloat16)


def seg_positions(seg_rows):
    positions = jnp.arange(seg_rows.shape[-1], dtype=jnp.int32)
    previous = jnp.concatenate([seg_rows[..., :1] - 1, seg_rows[..., :-1]], axis=-1)
    start_at = jnp.where(seg_rows != previous, positions, 0)
    return positions - lax.cummax(start_at, axis=seg_rows.ndim - 1)


def rope_tables(positions, head_dim):
    half_dim = head_dim // 2
    inv_freq = ROPE_BASE ** (-2.0 * jnp.arange(half_dim, dtype=jnp.float32) / head_dim)
    angles = positions.astype(jnp.float32)[..., None] * inv_freq
    return jnp.cos(angles), jnp.sin(angles)


def apply_rope(values, cos_t, sin_t):
    half_dim = values.shape[-1] // 2
    first_half = values[..., :half_dim]
    second_half = values[..., half_dim:]
    return jnp.concatenate([first_half * cos_t - second_half * sin_t, second_half * cos_t + first_half * sin_t], axis=-1)


def attend(q_rot, k_rot, v_val, allowed):
    scores = jnp.einsum('msngd,mtnd->mnsgt', q_rot, k_rot, preferred_element_type=jnp.float32) * q_rot.shape[-1] ** -0.5
    scores = jnp.where(allowed[:, None, :, None, :], scores, NEG_BIG)
    probs_bf = jax.nn.softmax(scores, axis=-1).astype(jnp.bfloat16)
    return jnp.einsum('mnsgt,mtnd->mnsgd', probs_bf, v_val, preferred_element_type=jnp.float32).astype(jnp.bfloat16)


def solution(mesh):
    act_spec = P(None, ('rep', 'tok', 'mp'), None)
    seg_spec = P(None, ('rep', 'tok', 'mp'))
    gain_spec = P(None, None)
    head_in = P(None, 'tok', 'mp', None)
    head_out = P(None, 'mp', None, 'tok')
    ffn_in = P(None, 'tok', 'mp')
    ffn_out = P(None, 'mp', 'tok')

    def device_fn(x_in, seg_ids, g_attn, w_q, w_k, w_v, w_o, g_mlp, w_gate, w_up, w_down):
        micro_n = x_in.shape[0]
        head_dim = w_q.shape[3]
        kv_heads = w_k.shape[2]
        groups = w_q.shape[2] // kv_heads
        seg_blk = lax.all_gather(seg_ids, 'mp', axis=1, tiled=True)
        blk_len = seg_blk.shape[1]
        tok_order = jnp.arange(blk_len)
        allowed = (seg_blk[:, :, None] == seg_blk[:, None, :]) & (tok_order[None, :] <= tok_order[:, None])
        cos_t, sin_t = rope_tables(seg_positions(seg_blk), head_dim)
        cos_t = cos_t[:, :, None, :]
        sin_t = sin_t[:, :, None, :]
        residual = x_in.astype(jnp.float32)
        for layer_idx in range(w_q.shape[0]):
            wq_full = lax.all_gather(w_q[layer_idx], 'tok', axis=0, tiled=True)
            wk_full = lax.all_gather(w_k[layer_idx], 'tok', axis=0, tiled=True)
            wv_full = lax.all_gather(w_v[layer_idx], 'tok', axis=0, tiled=True)
            wo_full = lax.all_gather(w_o[layer_idx], 'tok', axis=2, tiled=True)
            wg_full = lax.all_gather(w_gate[layer_idx], 'tok', axis=0, tiled=True)
            wu_full = lax.all_gather(w_up[layer_idx], 'tok', axis=0, tiled=True)
            wd_full = lax.all_gather(w_down[layer_idx], 'tok', axis=1, tiled=True)
            embed_dim = wo_full.shape[2]

            hidden = rms_norm(residual, g_attn[layer_idx])
            h_blk = lax.all_gather(hidden, 'mp', axis=1, tiled=True)
            q_lin = jnp.einsum('mse,end->msnd', h_blk, wq_full, preferred_element_type=jnp.float32)
            k_lin = jnp.einsum('mse,end->msnd', h_blk, wk_full, preferred_element_type=jnp.float32)
            v_val = jnp.einsum('mse,end->msnd', h_blk, wv_full, preferred_element_type=jnp.float32).astype(jnp.bfloat16)
            q_rot = apply_rope(q_lin, cos_t, sin_t).astype(jnp.bfloat16).reshape(micro_n, blk_len, kv_heads, groups, head_dim)
            k_rot = apply_rope(k_lin, cos_t, sin_t).astype(jnp.bfloat16)
            attn_out = attend(q_rot, k_rot, v_val, allowed)
            part_sum = jnp.einsum('mnsgd,ngde->mse', attn_out, wo_full.reshape(kv_heads, groups, head_dim, embed_dim), preferred_element_type=jnp.float32)
            residual = residual + lax.psum_scatter(part_sum, 'mp', scatter_dimension=1, tiled=True)

            hidden = rms_norm(residual, g_mlp[layer_idx])
            h_blk = lax.all_gather(hidden, 'mp', axis=1, tiled=True)
            gate_val = jnp.einsum('mse,ef->msf', h_blk, wg_full, preferred_element_type=jnp.float32)
            up_val = jnp.einsum('mse,ef->msf', h_blk, wu_full, preferred_element_type=jnp.float32)
            act_val = (jax.nn.silu(gate_val) * up_val).astype(jnp.bfloat16)
            part_sum = jnp.einsum('msf,fe->mse', act_val, wd_full, preferred_element_type=jnp.float32)
            residual = residual + lax.psum_scatter(part_sum, 'mp', scatter_dimension=1, tiled=True)
        return residual

    return jax.shard_map(
        device_fn,
        mesh=mesh,
        in_specs=(act_spec, seg_spec, gain_spec, head_in, head_in, head_in, head_out, gain_spec, ffn_in, ffn_in, ffn_out),
        out_specs=act_spec,
        check_vma=False,
    )
```

profile of v0, /device:TPU:0, one launch (start us, length us, event | category | flops | bytes accessed | tf_op | source)
XLA Modules:
  0.0 4283.9 jit_solution(10756541674703408811)
XLA Ops:
  6.5 1.4 slice_convert_fusion.1
  8.0 1.7 fusion.62
  9.7 2.8 fusion.64
  12.5 10.4 fusion.148
  22.9 9.5 copy.51
  32.5 10.4 fusion.149
  42.9 9.5 copy.50
  52.5 10.4 fusion.150
  62.9 9.5 fusion.151
  73.0 5.7 all-gather.14
  79.8 132.0 %all-gather.44.cloned.1.call-done = bf16[1,5120,20,128]{1,3,2,0:T(8,128)(2,1)} async-done(((bf16[1,1280,20,128]{1,3,2,0:T(8,128)(2,1)}), bf16[1,5120,20,128]{1,3,2,0:T(8,128)(2,1)}) %all-gather.44.cloned.1.call-update) | async-done | bytes 26214416 | tf_op jit(solution)/shard_map/all_gather | solution.py:68
  211.8 12.5 fusion.26
  224.2 147.7 %all-gather.42.cloned.1.call-done = bf16[1,5120,20,128]{1,3,2,0:T(8,128)(2,1)} async-done(((bf16[1,1280,20,128]{1,3,2,0:T(8,128)(2,1)}), bf16[1,5120,20,128]{1,3,2,0:T(8,128)(2,1)}) %all-gather.42.cloned.1.call-update) | async-done | bytes 26214416 | tf_op jit(solution)/shard_map/all_gather | solution.py:67
  372.0 12.5 fusion.28
  384.5 2.0 subtract_convert_fusion.2
  386.5 4.2 fusion.152
  390.7 141.0 %all-gather.46.cloned.1.call-done = bf16[1,5120,20,128]{3,1,2,0:T(8,128)(2,1)} async-done(((bf16[1,1280,20,128]{3,1,2,0:T(8,128)(2,1)}), bf16[1,5120,20,128]{3,1,2,0:T(8,128)(2,1)}) %all-gather.46.cloned.1.call-update) | async-done | bytes 26214416 | tf_op jit(solution)/shard_map/all_gather | solution.py:69
  531.7 13.3 fusion.73
  545.0 146.7 %all-gather.48.cloned.1.call-done = bf16[1,20,128,5120]{3,2,1,0:T(8,128)(2,1)} async-done(((bf16[1,20,128,1280]{3,2,1,0:T(8,128)(2,1)}), bf16[1,20,128,5120]{3,2,1,0:T(8,128)(2,1)}) %all-gather.48.cloned.1.call-update) | async-done | bytes 26214416 | tf_op jit(solution)/shard_map/all_gather | solution.py:70
  691.7 15.4 fusion.54
  707.9 0.6 slice_convert_fusion
  708.5 61.7 %reduce-scatter.5.cloned.1.call-done = f32[2,64,5120]{2,1,0:T(8,128)} async-done(((f32[2,128,5120]{2,1,0:T(8,128)}), f32[2,64,5120]{2,1,0:T(8,128)}) %reduce-scatter.5.cloned.1.call-update) | async-done | bytes 2621456 | tf_op jit(solution)/shard_map/reduce_scatter | solution.py:85
  770.2 2.3 multiply_reduce_fusion.2
  772.8 1.5 multiply_convert_fusion.2
  774.4 25.9 fusion.145
  800.4 26.0 fusion.146
  826.4 25.6 fusion.147
  852.1 372.3 %all-gather.50.cloned.1.call-done = bf16[1,5120,6912]{2,1,0:T(8,128)(2,1)} async-done(((bf16[1,1280,6912]{2,1,0:T(8,128)(2,1)}), bf16[1,5120,6912]{2,1,0:T(8,128)(2,1)}) %all-gather.50.cloned.1.call-update) | async-done | bytes 70778896 | tf_op jit(solution)/shard_map/all_gather | solution.py:71
  1224.5 32.0 fusion.12
  1256.5 381.8 %all-gather.52.cloned.1.call-done = bf16[1,5120,6912]{2,1,0:T(8,128)(2,1)} async-done(((bf16[1,1280,6912]{2,1,0:T(8,128)(2,1)}), bf16[1,5120,6912]{2,1,0:T(8,128)(2,1)}) %all-gather.52.cloned.1.call-update) | async-done | bytes 70778896 | tf_op jit(solution)/shard_map/all_gather | solution.py:72
  1638.3 32.0 fusion.39.clone.2
  1670.3 381.6 %all-gather.54.cloned.1.call-done = bf16[1,6912,5120]{2,1,0:T(8,128)(2,1)} async-done(((bf16[1,6912,1280]{2,1,0:T(8,128)(2,1)}), bf16[1,6912,5120]{2,1,0:T(8,128)(2,1)}) %all-gather.54.cloned.1.call-update) | async-done | bytes 70778896 | tf_op jit(solution)/shard_map/all_gather | solution.py:73
  2051.9 30.1 fusion.8
  2082.1 9.4 copy.52
  2091.6 53.5 %reduce-scatter.7.cloned.1.call-done = f32[2,64,5120]{2,1,0:T(8,128)} async-done(((f32[2,128,5120]{2,1,0:T(8,128)}), f32[2,64,5120]{2,1,0:T(8,128)}) %reduce-scatter.7.cloned.1.call-update) | async-done | bytes 2621456 | tf_op jit(solution)/shard_map/reduce_scatter | solution.py:93
  2145.1 3.1 multiply_reduce_fusion.1
  2148.1 1.5 copy-done.2
  2149.6 1.4 multiply_convert_fusion.1
  2151.1 9.5 copy.53
  2161.8 143.3 %all-gather.56.cloned.1.call-done = bf16[1,5120,20,128]{1,3,2,0:T(8,128)(2,1)} async-done(((bf16[1,1280,20,128]{1,3,2,0:T(8,128)(2,1)}), bf16[1,5120,20,128]{1,3,2,0:T(8,128)(2,1)}) %all-gather.56.cloned.1.call-update) | async-done | bytes 26214416 | tf_op jit(solution)/shard_map/all_gather | solution.py:67
  2305.1 37.7 all-gather.38.cloned.1.call-done
  2342.8 12.7 fusion.20
  2355.5 147.3 %all-gather.58.cloned.1.call-done = bf16[1,5120,20,128]{1,3,2,0:T(8,128)(2,1)} async-done(((bf16[1,1280,20,128]{1,3,2,0:T(8,128)(2,1)}), bf16[1,5120,20,128]{1,3,2,0:T(8,128)(2,1)}) %all-gather.58.cloned.1.call-update) | async-done | bytes 26214416 | tf_op jit(solution)/shard_map/all_gather | solution.py:68
  2502.9 12.5 fusion.18
  2515.4 2.0 subtract_convert_fusion
  2517.4 4.2 fusion.157
  2521.6 141.0 %all-gather.60.cloned.1.call-done = bf16[1,5120,20,128]{3,1,2,0:T(8,128)(2,1)} async-done(((bf16[1,1280,20,128]{3,1,2,0:T(8,128)(2,1)}), bf16[1,5120,20,128]{3,1,2,0:T(8,128)(2,1)}) %all-gather.60.cloned.1.call-update) | async-done | bytes 26214416 | tf_op jit(solution)/shard_map/all_gather | solution.py:69
  2662.6 13.3 fusion.78
  2675.8 146.8 %all-gather.62.cloned.1.call-done = bf16[1,20,128,5120]{3,2,1,0:T(8,128)(2,1)} async-done(((bf16[1,20,128,1280]{3,2,1,0:T(8,128)(2,1)}), bf16[1,20,128,5120]{3,2,1,0:T(8,128)(2,1)}) %all-gather.62.cloned.1.call-update) | async-done | bytes 26214416 | tf_op jit(solution)/shard_map/all_gather | solution.py:70
  2822.6 15.5 fusion.57
  2838.8 62.4 %reduce-scatter.9.cloned.1.call-done = f32[2,64,5120]{2,1,0:T(8,128)} async-done(((f32[2,128,5120]{2,1,0:T(8,128)}), f32[2,64,5120]{2,1,0:T(8,128)}) %reduce-scatter.9.cloned.1.call-update) | async-done | bytes 2621456 | tf_op jit(solution)/shard_map/reduce_scatter | solution.py:85
  2901.2 2.1 multiply_reduce_fusion
  2903.3 1.5 copy-done.5
  2904.8 1.4 multiply_convert_fusion
  2906.8 0.7 all-gather.68.cloned.1.call-update
  2907.6 407.3 %all-gather.64.cloned.1.call-done = bf16[1,5120,6912]{2,1,0:T(8,128)(2,1)} async-done(((bf16[1,1280,6912]{2,1,0:T(8,128)(2,1)}), bf16[1,5120,6912]{2,1,0:T(8,128)(2,1)}) %all-gather.64.cloned.1.call-update) | async-done | bytes 70778896 | tf_op jit(solution)/shard_map/all_gather | solution.py:71
  3314.8 37.7 all-gather.40.cloned.1.call-done
  3352.5 39.0 fusion.6
  3391.5 374.7 %all-gather.66.cloned.1.call-done = bf16[1,5120,6912]{2,1,0:T(8,128)(2,1)} async-done(((bf16[1,1280,6912]{2,1,0:T(8,128)(2,1)}), bf16[1,5120,6912]{2,1,0:T(8,128)(2,1)}) %all-gather.66.cloned.1.call-update) | async-done | bytes 70778896 | tf_op jit(solution)/shard_map/all_gather | solution.py:72
  3766.2 32.2 fusion.36.clone.4
  3798.4 381.6 %all-gather.68.cloned.1.call-done = bf16[1,6912,5120]{2,1,0:T(8,128)(2,1)} async-done(((bf16[1,6912,1280]{2,1,0:T(8,128)(2,1)}), bf16[1,6912,5120]{2,1,0:T(8,128)(2,1)}) %all-gather.68.cloned.1.call-update) | async-done | bytes 70778896 | tf_op jit(solution)/shard_map/all_gather | solution.py:73
  4180.0 30.2 fusion.2
  4210.2 63.0 %reduce-scatter.11.cloned.1.call-done = f32[2,64,5120]{2,1,0:T(8,128)} async-done(((f32[2,128,5120]{2,1,0:T(8,128)}), f32[2,64,5120]{2,1,0:T(8,128)}) %reduce-scatter.11.cloned.1.call-update) | async-done | bytes 2621456 | tf_op jit(solution)/shard_map/reduce_scatter | solution.py:93
  4273.3 3.5 add.85
  (99 shorter events, 5.7 us)
Async XLA Ops:
  6.5 73.2 %all-gather.34.cloned.1.call-start = ((), (), s32[]{:S(2)}) async-start(), calls=%async_computation.4 | async-start | bytes 3932160 | tf_op jit(solution)/shard_map/all_gather | solution.py:77
  12.4 199.3 %all-gather.44.cloned.1.call-start = ((), (), s32[]{:S(2)}) async-start(), calls=%async_computation.13 | async-start | bytes 32768000 | tf_op jit(solution)/shard_map/all_gather | solution.py:68
  32.5 339.5 %all-gather.42.cloned.1.call-start = ((), (), s32[]{:S(2)}) async-start(), calls=%async_computation.12 | async-start | bytes 32768000 | tf_op jit(solution)/shard_map/all_gather | solution.py:67
  52.4 479.3 %all-gather.46.cloned.1.call-start = ((), (), s32[]{:S(2)}) async-start(), calls=%async_computation.14 | async-start | bytes 32768000 | tf_op jit(solution)/shard_map/all_gather | solution.py:69
  62.8 628.9 %all-gather.48.cloned.1.call-start = ((), (), s32[]{:S(2)}) async-start(), calls=%async_computation.15 | async-start | bytes 32768000 | tf_op jit(solution)/shard_map/all_gather | solution.py:70
  72.4 0.7 copy-start.16
  72.4 697.8 %reduce-scatter.5.cloned.1.call-start = ((), (), s32[]{:S(2)}) async-start(), calls=%async_computation.5 | async-start | bytes 7864320 | tf_op jit(solution)/shard_map/reduce_scatter | solution.py:85
  79.4 307.1 %copy-start.14 = (pred[2,128,128]{1,2,0:T(8,128)(4,1)}, pred[2,128,128]{1,2,0:T(8,128)(4,1)S(1)}, u32[]{:S(2)}) copy-start(pred[2,128,128]{1,2,0:T(8,128)(4,1)S(1)} %compare_and_fusion) | copy-start | bytes 98308
  79.7 304.7 %copy-start.7 = (f32[2,128,64]{1,2,0:T(8,128)}, f32[2,128,64]{1,2,0:T(8,128)S(1)}, u32[]{:S(2)}) copy-start(f32[2,128,64]{1,2,0:T(8,128)S(1)} %get-tuple-element.39) | copy-start | bytes 196612
  79.8 304.7 %copy-start.9 = (f32[2,128,64]{1,2,0:T(8,128)}, f32[2,128,64]{1,2,0:T(8,128)S(1)}, u32[]{:S(2)}) copy-start(f32[2,128,64]{1,2,0:T(8,128)S(1)} %get-tuple-element.40) | copy-start | bytes 196612
  386.5 145.2 %copy-start.17 = (bf16[2,128,5120]{2,1,0:T(8,128)(2,1)S(1)}, bf16[2,128,5120]{2,1,0:T(8,128)(2,1)}, u32[]{:S(2)}) copy-start(bf16[2,128,5120]{2,1,0:T(8,128)(2,1)} %all-gather.34.cloned.1.call-done) | copy-start | bytes 7864324
  707.2 0.7 copy-start.13
  707.2 63.1 %copy-start = (bf16[2,64,5120]{2,1,0:T(8,128)(2,1)S(1)}, bf16[2,64,5120]{2,1,0:T(8,128)(2,1)}, u32[]{:S(2)}) copy-start(bf16[2,64,5120]{2,1,0:T(8,128)(2,1)} %param.11) | copy-start | bytes 3932164
  707.2 144.9 %all-gather.36.cloned.1.call-start = ((), (), s32[]{:S(2)}) async-start(), calls=%async_computation.6 | async-start | bytes 3932160 | tf_op jit(solution)/shard_map/all_gather | solution.py:88
  770.2 2.5 copy-start.4
  774.3 450.1 %all-gather.50.cloned.1.call-start = ((), (), s32[]{:S(2)}) async-start(), calls=%async_computation.16 | async-start | bytes 88473600 | tf_op jit(solution)/shard_map/all_gather | solution.py:71
  800.3 838.0 %all-gather.52.cloned.1.call-start = ((), (), s32[]{:S(2)}) async-start(), calls=%async_computation.17 | async-start | bytes 88473600 | tf_op jit(solution)/shard_map/all_gather | solution.py:72
  826.4 1225.5 %all-gather.54.cloned.1.call-start = ((), (), s32[]{:S(2)}) async-start(), calls=%async_computation.18 | async-start | bytes 88473600 | tf_op jit(solution)/shard_map/all_gather | solution.py:73
  852.0 1293.0 %reduce-scatter.7.cloned.1.call-start = ((), (), s32[]{:S(2)}) async-start(), calls=%async_computation.7 | async-start | bytes 7864320 | tf_op jit(solution)/shard_map/reduce_scatter | solution.py:93
  852.1 786.2 %copy-start.19 = (bf16[2,128,5120]{2,1,0:T(8,128)(2,1)S(1)}, bf16[2,128,5120]{2,1,0:T(8,128)(2,1)}, u32[]{:S(2)}) copy-start(bf16[2,128,5120]{2,1,0:T(8,128)(2,1)} %all-gather.36.cloned.1.call-done) | copy-start | bytes 7864324
  2082.0 223.1 %all-gather.56.cloned.1.call-start = ((), (), s32[]{:S(2)}) async-start(), calls=%async_computation.19 | async-start | bytes 32768000 | tf_op jit(solution)/shard_map/all_gather | solution.py:67
  2091.5 53.6 %copy-start.1 = (bf16[2,64,5120]{2,1,0:T(8,128)(2,1)S(1)}, bf16[2,64,5120]{2,1,0:T(8,128)(2,1)}, u32[]{:S(2)}) copy-start(bf16[2,64,5120]{2,1,0:T(8,128)(2,1)} %param.11) | copy-start | bytes 3932164
  2091.5 58.1 %copy-start.11 = (f32[1,5120]{1,0:T(1,128)S(1)}, f32[1,5120]{1,0:T(1,128)}, u32[]{:S(2)}) copy-start(f32[1,5120]{1,0:T(1,128)} %get-tuple-element.37) | copy-start | bytes 61444
  2091.5 251.3 %all-gather.38.cloned.1.call-start = ((), (), s32[]{:S(2)}) async-start(), calls=%async_computation.8 | async-start | bytes 3932160 | tf_op jit(solution)/shard_map/all_gather | solution.py:77
  2148.1 1.5 copy-start.2
  2151.0 351.8 %all-gather.58.cloned.1.call-start = ((), (), s32[]{:S(2)}) async-start(), calls=%async_computation.20 | async-start | bytes 32768000 | tf_op jit(solution)/shard_map/all_gather | solution.py:68
  2160.6 502.0 %all-gather.60.cloned.1.call-start = ((), (), s32[]{:S(2)}) async-start(), calls=%async_computation.21 | async-start | bytes 32768000 | tf_op jit(solution)/shard_map/all_gather | solution.py:69
  2161.2 661.4 %all-gather.62.cloned.1.call-start = ((), (), s32[]{:S(2)}) async-start(), calls=%async_computation.22 | async-start | bytes 32768000 | tf_op jit(solution)/shard_map/all_gather | solution.py:70
  2161.8 739.4 %reduce-scatter.9.cloned.1.call-start = ((), (), s32[]{:S(2)}) async-start(), calls=%async_computation.9 | async-start | bytes 7864320 | tf_op jit(solution)/shard_map/reduce_scatter | solution.py:85
  2355.5 159.8 %copy-start.8 = (f32[2,128,64]{1,2,0:T(8,128)S(1)}, f32[2,128,64]{1,2,0:T(8,128)}, u32[]{:S(2)}) copy-start(f32[2,128,64]{1,2,0:T(8,128)} %copy-done.7) | copy-start | bytes 196612
  2355.5 159.8 %copy-start.10 = (f32[2,128,64]{1,2,0:T(8,128)S(1)}, f32[2,128,64]{1,2,0:T(8,128)}, u32[]{:S(2)}) copy-start(f32[2,128,64]{1,2,0:T(8,128)} %copy-done.9) | copy-start | bytes 196612
  2515.4 2.0 copy-start.15
  2517.4 145.2 %copy-start.18 = (bf16[2,128,5120]{2,1,0:T(8,128)(2,1)S(1)}, bf16[2,128,5120]{2,1,0:T(8,128)(2,1)}, u32[]{:S(2)}) copy-start(bf16[2,128,5120]{2,1,0:T(8,128)(2,1)} %all-gather.38.cloned.1.call-done) | copy-start | bytes 7864324
  2838.1 476.7 %all-gather.64.cloned.1.call-start = ((), (), s32[]{:S(2)}) async-start(), calls=%async_computation.23 | async-start | bytes 88473600 | tf_op jit(solution)/shard_map/all_gather | solution.py:71
  2838.2 63.0 %copy-start.3 = (f32[2,64,5120]{2,1,0:T(8,128)S(1)}, f32[2,64,5120]{2,1,0:T(8,128)}, u32[]{:S(2)}) copy-start(f32[2,64,5120]{2,1,0:T(8,128)} %copy-done.2) | copy-start | bytes 7864324
  2838.7 66.1 %copy-start.12 = (f32[1,5120]{1,0:T(1,128)S(1)}, f32[1,5120]{1,0:T(1,128)}, u32[]{:S(2)}) copy-start(f32[1,5120]{1,0:T(1,128)} %get-tuple-element.35) | copy-start | bytes 61444
  2838.7 513.8 %all-gather.40.cloned.1.call-start = ((), (), s32[]{:S(2)}) async-start(), calls=%async_computation.10 | async-start | bytes 3932160 | tf_op jit(solution)/shard_map/all_gather | solution.py:88
  2903.3 1.5 copy-start.5
  2906.2 860.0 %all-gather.66.cloned.1.call-start = ((), (), s32[]{:S(2)}) async-start(), calls=%async_computation.24 | async-start | bytes 88473600 | tf_op jit(solution)/shard_map/all_gather | solution.py:72
  2906.8 1273.2 %all-gather.68.cloned.1.call-start = ((), (), s32[]{:S(2)}) async-start(), calls=%async_computation.25 | async-start | bytes 88473600 | tf_op jit(solution)/shard_map/all_gather | solution.py:73
  2907.5 1365.7 %reduce-scatter.11.cloned.1.call-start = ((), (), s32[]{:S(2)}) async-start(), calls=%async_computation.11 | async-start | bytes 7864320 | tf_op jit(solution)/shard_map/reduce_scatter | solution.py:93
  3352.5 413.7 %copy-start.20 = (bf16[2,128,5120]{2,1,0:T(8,128)(2,1)S(1)}, bf16[2,128,5120]{2,1,0:T(8,128)(2,1)}, u32[]{:S(2)}) copy-start(bf16[2,128,5120]{2,1,0:T(8,128)(2,1)} %all-gather.40.cloned.1.call-done) | copy-start | bytes 7864324
  4210.2 63.1 %copy-start.6 = (f32[2,64,5120]{2,1,0:T(8,128)S(1)}, f32[2,64,5120]{2,1,0:T(8,128)}, u32[]{:S(2)}) copy-start(f32[2,64,5120]{2,1,0:T(8,128)} %copy-done.5) | copy-start | bytes 7864324
Sparse Core Ops, SparseCore 0:
  12.6 38.9 all-gather.33
  53.1 158.6 all-gather.43
  213.3 158.6 all-gather.41
  373.4 158.2 all-gather.45
  533.1 158.6 all-gather.47
  707.3 62.8 reduce-scatter.4
  774.4 36.1 all-gather.35
  812.2 412.2 all-gather.49
  1226.0 412.2 all-gather.51
  1639.7 412.1 all-gather.53
  2082.1 62.8 reduce-scatter.6
  2146.4 158.6 all-gather.55
  2306.6 36.1 all-gather.37
  2344.2 158.6 all-gather.57
  2504.3 158.2 all-gather.59
  2663.9 158.6 all-gather.61
  2838.2 62.8 reduce-scatter.8
  2902.6 412.2 all-gather.63
  3316.3 36.1 all-gather.39
  3353.9 412.2 all-gather.65
  3767.7 412.1 all-gather.67
  4210.3 62.8 reduce-scatter.10
where the time goes:
time: 4290 us; the launch traced here: 4280 us
  waiting for transfers between devices  3760 us (88%)
  matrix products  311 us (7%)
  local copies, waits for them, and re-layouts  160 us (4%)
    all_gather x2, waiting for transfers between devices, device_fn(): wg_full = lax.all_gather(w_gate[layer_idx], 'tok', axis=0, tiled=True)  780 us
    all_gather x2, waiting for transfers between devices, device_fn(): wd_full = lax.all_gather(w_down[layer_idx], 'tok', axis=1, tiled=True)  763 us
    all_gather x2, waiting for transfers between devices, device_fn(): wu_full = lax.all_gather(w_up[layer_idx], 'tok', axis=0, tiled=True)  757 us
    all_gather x2, waiting for transfers between devices, device_fn(): wo_full = lax.all_gather(w_o[layer_idx], 'tok', axis=2, tiled=True)  294 us
    all_gather x2, waiting for transfers between devices, device_fn(): wq_full = lax.all_gather(w_q[layer_idx], 'tok', axis=0, tiled=True)  291 us
    all_gather x2, waiting for transfers between devices, device_fn(): wv_full = lax.all_gather(w_v[layer_idx], 'tok', axis=0, tiled=True)  282 us
    all_gather x2, waiting for transfers between devices, device_fn(): wk_full = lax.all_gather(w_k[layer_idx], 'tok', axis=0, tiled=True)  279 us
    reduce_scatter x4, waiting for transfers between devices, device_fn(): lax.psum_scatter(part_sum, 'mp', scatter_dimension=1, tiled=True)  241 us
  transfers between devices with their start and end apart: 22, of which 20 were waited for; matrix products, arithmetic and copies ran while one was open for 9% of the time, Pallas kernels for 0%

commit v1 on v0

v1 whole, which is shorter than its diff:
```python
import jax
import jax.numpy as jnp
from jax import lax
from jax.sharding import PartitionSpec as P

NORM_EPS = 1e-5
ROPE_BASE = 10000.0
NEG_BIG = -1e30
F32 = jnp.float32
BF16 = jnp.bfloat16


def seg_positions(seg_rows):
    positions = jnp.arange(seg_rows.shape[-1], dtype=jnp.int32)
    previous = jnp.concatenate([seg_rows[..., :1] - 1, seg_rows[..., :-1]], axis=-1)
    start_at = jnp.where(seg_rows != previous, positions, 0)
    return positions - lax.cummax(start_at, axis=seg_rows.ndim - 1)


def rope_tables(positions, head_dim):
    half_dim = head_dim // 2
    inv_freq = ROPE_BASE ** (-2.0 * jnp.arange(half_dim, dtype=F32) / head_dim)
    angles = positions.astype(F32)[..., None] * inv_freq
    return jnp.cos(angles), jnp.sin(angles)


def apply_rope(values, cos_t, sin_t):
    half_dim = values.shape[-1] // 2
    a = values[..., :half_dim]
    b = values[..., half_dim:]
    return jnp.concatenate([a * cos_t - b * sin_t, b * cos_t + a * sin_t], axis=-1)


def dot(a, b):
    return lax.dot_general(a, b, (((a.ndim - 1,), (0,)), ((), ())), preferred_element_type=F32)


GU_CHUNKS = 3


def solution(mesh):
    act_spec = P(None, ('rep', 'tok', 'mp'), None)
    seg_spec = P(None, ('rep', 'tok', 'mp'))
    gain_spec = P(None, None)
    head_in = P(None, 'tok', 'mp', None)
    head_out = P(None, 'mp', None, 'tok')
    ffn_in = P(None, 'tok', 'mp')
    ffn_out = P(None, 'mp', 'tok')

    def to_x(v):
        return lax.ppermute(v, 'tok', [(i, i ^ 2) for i in range(4)])

    def to_c(v):
        return lax.ppermute(v, 'tok', [(i, i ^ 1) for i in range(4)])

    def to_xc(v):
        return lax.ppermute(v, 'tok', [(i, i ^ 3) for i in range(4)])

    def to_y(v):
        return lax.ppermute(v, 'mp', [(0, 1), (1, 0)])

    def device_fn(x_in, seg_ids, g_attn, w_q, w_k, w_v, w_o, g_mlp, w_gate, w_up, w_down):
        n_layers = w_q.shape[0]
        micro_n, loc_len, embed = x_in.shape
        feat = w_q.shape[1]
        heads, head_dim = w_q.shape[2], w_q.shape[3]
        h_half = heads // 2
        ffn = w_gate.shape[2]
        f_half = ffn // 2
        f_chunk = f_half // GU_CHUNKS
        t = lax.axis_index('tok')
        m = lax.axis_index('mp')
        core = t % 2
        xpos = t // 2

        seg_all = lax.all_gather(seg_ids, ('tok', 'mp'), axis=1, tiled=True)
        blk_len = 2 * loc_len
        seg_own = lax.dynamic_slice_in_dim(seg_all, xpos * 2 * blk_len, 2 * blk_len, 1).reshape(micro_n, 2, blk_len)
        pos_own = seg_positions(seg_own)
        in_blk = jnp.broadcast_to(jnp.arange(blk_len, dtype=jnp.int32), seg_own.shape)
        def half_first(v):
            v4 = v.reshape(micro_n, 2, 2, loc_len)
            return jnp.where(m == 0, v4, v4[:, :, ::-1]).reshape(micro_n, 2, blk_len)
        seg_own, pos_own, in_blk = half_first(seg_own), half_first(pos_own), half_first(in_blk)
        allowed = (seg_own[..., :, None] == seg_own[..., None, :]) & (in_blk[..., None, :] <= in_blk[..., :, None])
        cos_t, sin_t = rope_tables(pos_own, head_dim)

        def to_rows(v):
            d = v.shape[-1]
            return v.reshape(micro_n, 2, 2, loc_len, d).transpose(0, 2, 1, 3, 4).reshape(micro_n, 2 * blk_len, 1, d)
        cos_t, sin_t = to_rows(cos_t), to_rows(sin_t)

        def start_piece(mb, k):
            s = lax.dynamic_slice_in_dim(x_in[mb], (t ^ k) * feat, feat, 1)
            return s
        resid = []
        for mb in range(micro_n):
            p = [start_piece(mb, 0), to_c(start_piece(mb, 1)), to_x(start_piece(mb, 2)), to_xc(start_piece(mb, 3))]
            own = jnp.where(core == 0, jnp.stack([p[0], p[1]]), jnp.stack([p[1], p[0]]))
            oth = jnp.where(core == 0, jnp.stack([p[2], p[3]]), jnp.stack([p[3], p[2]]))
            resid.append(jnp.stack([own, oth]).astype(F32))

        def normed(r, gain):
            sq = jnp.sum(r * r, axis=-1)
            sq = sq + to_c(sq)
            sq = sq + to_x(sq)[::-1]
            scale = lax.rsqrt(sq / embed + NORM_EPS)
            g = lax.dynamic_slice_in_dim(gain, t * feat, feat, 0).astype(F32)
            h_loc = (r * scale[..., None] * g).astype(BF16)
            h_y = to_y(h_loc)
            h = jnp.stack([h_loc, h_y], axis=1).reshape(2, 2 * blk_len, feat)
            h_c = to_c(h)
            return h, h_c

        def swap_halves(w, half):
            own = lax.dynamic_slice_in_dim(w, core * half, half, 1)
            snd = lax.dynamic_slice_in_dim(w, (1 - core) * half, half, 1)
            return own, to_c(snd)

        def col_matmul(h, h_c, w_own, w_rcv):
            snd = dot(h[1], w_own) + dot(h_c[1], w_rcv)
            got = to_x(snd)
            return dot(h[0], w_own) + dot(h_c[0], w_rcv) + got

        def row_reduce(parts):
            half = blk_len
            snd = keep = None
            for a_own, a_oth, w in parts:
                mine = jnp.concatenate([a_own[:half], a_oth[:half]], axis=0)
                theirs = jnp.concatenate([a_own[half:], a_oth[half:]], axis=0)
                d_snd, d_keep = dot(theirs, w), dot(mine, w)
                snd = d_snd if snd is None else snd + d_snd
                keep = d_keep if keep is None else keep + d_keep
            return (keep + to_y(snd)).reshape(2, 2, loc_len, feat)

        for l in range(n_layers):
            qkv_w = []
            for w in (w_k, w_v, w_q):
                own, rcv = swap_halves(w[l], h_half)
                qkv_w.append((own.reshape(feat, -1), rcv.reshape(feat, -1)))
            gu_w = [swap_halves(w[l], f_half) for w in (w_gate, w_up)]
            wo = w_o[l].reshape(heads * head_dim, feat)
            hd = h_half * head_dim
            wo_own = lax.dynamic_slice_in_dim(wo, core * hd, hd, 0)
            wo_oth = lax.dynamic_slice_in_dim(wo, (1 - core) * hd, hd, 0)

            for mb in range(micro_n):
                h, h_c = normed(resid[mb], g_attn[l])
                k_lin, v_lin, q_lin = [col_matmul(h, h_c, *w).reshape(2 * blk_len, h_half, head_dim) for w in qkv_w]
                k_rot = apply_rope(k_lin, cos_t[mb], sin_t[mb]).astype(BF16)
                q_rot = apply_rope(q_lin, cos_t[mb], sin_t[mb]).astype(BF16)
                v_val = v_lin.astype(BF16)

                def blocks(v):
                    return v.reshape(2, 2, loc_len, h_half, head_dim).transpose(1, 0, 2, 3, 4).reshape(2, blk_len, h_half, head_dim)
                qb, kb, vb = blocks(q_rot), blocks(k_rot), blocks(v_val)
                scores = jnp.einsum('bsnd,btnd->bnst', qb, kb, preferred_element_type=F32) * head_dim ** -0.5
                scores = jnp.where(allowed[mb][:, None], scores, NEG_BIG)
                probs = jax.nn.softmax(scores, axis=-1).astype(BF16)
                o = jnp.einsum('bnst,btnd->bsnd', probs, vb, preferred_element_type=F32).astype(BF16)
                o = o.reshape(2, 2, loc_len, hd).transpose(1, 0, 2, 3).reshape(2 * blk_len, hd)
                o_x = to_x(o)
                o_c = to_c(o)
                o_xc = to_c(o_x)
                resid[mb] = resid[mb] + row_reduce([(o, o_x, wo_own), (o_c, o_xc, wo_oth)])

            for mb in range(micro_n):
                h, h_c = normed(resid[mb], g_mlp[l])
                parts = []
                for j in range(GU_CHUNKS):
                    sl = slice(j * f_chunk, (j + 1) * f_chunk)
                    gate, up = [col_matmul(h, h_c, w_own[:, sl], w_rcv[:, sl]) for w_own, w_rcv in gu_w]
                    act = (jax.nn.silu(gate) * up).astype(BF16)
                    a_x = to_x(act)
                    a_c = to_c(act)
                    a_xc = to_c(a_x)
                    wd_own = lax.dynamic_slice_in_dim(w_down[l], core * f_half + j * f_chunk, f_chunk, 0)
                    wd_oth = lax.dynamic_slice_in_dim(w_down[l], (1 - core) * f_half + j * f_chunk, f_chunk, 0)
                    parts += [(act, a_x, wd_own), (a_c, a_xc, wd_oth)]
                resid[mb] = resid[mb] + row_reduce(parts)

        outs = []
        for mb in range(micro_n):
            r = resid[mb]
            r = jnp.where(core == 0, r, r[:, ::-1])
            p = [r[0, 0], to_c(r[0, 1]), to_x(r[1, 0]), to_xc(r[1, 1])]
            row = jnp.zeros((loc_len, embed), F32)
            for k in range(4):
                row = lax.dynamic_update_slice_in_dim(row, p[k], (t ^ k) * feat, 1)
            outs.append(row)
        return jnp.stack(outs)

    return jax.shard_map(
        device_fn,
        mesh=mesh,
        in_specs=(act_spec, seg_spec, gain_spec, head_in, head_in, head_in, head_out, gain_spec, ffn_in, ffn_in, ffn_out),
        out_specs=act_spec,
        check_vma=False,
    )
```

time: 4290 us -> 2100 us (0.49)
  waiting for transfers between devices: 3760 us -> 1050 us
  local copies, waits for them, and re-layouts: 160 us -> 422 us
  matrix products: 311 us -> 446 us
  starting transfers between devices: 1.27 us -> 107 us
    all_gather x18 -> x0, waiting for transfers between devices: 3520 us -> none  [the longest x2 780 us: device_fn(): wg_full = lax.all_gather(w_gate[layer_idx], 'tok', axis=0, tiled=True)]
    ppermute x0 -> x146, waiting for transfers between devices: none -> 1050 us  [the longest x64 781 us: to_x(): return lax.ppermute(v, 'tok', [(i, i ^ 2) for i in range(4)])]
    reduce_scatter x4 -> x0, waiting for transfers between devices: 241 us -> none  [device_fn(): lax.psum_scatter(part_sum, 'mp', scatter_dimension=1, tiled=True)]
    dot_general x14 -> x216, matrix products: 303 us -> 446 us  [the longest x208 430 us: dot(): lax.dot_general(a, b, (((a.ndim - 1,), (0,)), ((), ())), preferred_elemen...]
    ppermute x0 -> x146, starting transfers between devices: none -> 107 us  [the longest x64 73.6 us: to_x(): return lax.ppermute(v, 'tok', [(i, i ^ 2) for i in range(4)])]
    dynamic_slice x0 -> x11, local copies, waits for them, and re-layouts: none -> 71.2 us  [the longest x10 71.2 us: swap_halves(): snd = lax.dynamic_slice_in_dim(w, (1 - core) * half, half, 1)]
    concatenate x0 -> x32, local copies, waits for them, and re-layouts: none -> 65.9 us  [apply_rope(): jnp.concatenate([a * cos_t - b * sin_t, b * cos_t + a * sin_t], axis=-1)]
    slice x7 -> x76, local copies, waits for them, and re-layouts: 118 us -> 141 us  [the longest x2 51.7 us: device_fn(): gu_w = [swap_halves(w[l], f_half) for w in (w_gate, w_up)]]
  transfers between devices with their start and end apart: 22 -> 146, of which waited for: 20 -> 62; matrix products, arithmetic and copies ran while one was open for 9% -> 43% of each run, Pallas kernels for 0% -> 0%
where the time goes in v1:
time: 2100 us; the launch traced here: 2080 us
  waiting for transfers between devices  1050 us (50%)
  matrix products  446 us (21%)
  local copies, waits for them, and re-layouts  422 us (20%)
  starting transfers between devices  107 us (5%)
  other arithmetic  42.2 us (2%)
    ppermute x64, waiting for transfers between devices, to_x(): return lax.ppermute(v, 'tok', [(i, i ^ 2) for i in range(4)])  781 us
    dot_general x208, matrix products, dot(): lax.dot_general(a, b, (((a.ndim - 1,), (0,)), ((), ())), preferred_elemen...  430 us
    ppermute x16, waiting for transfers between devices, to_y(): return lax.ppermute(v, 'mp', [(0, 1), (1, 0)])  251 us
    unnamed x295, local copies, waits for them, and re-layouts  82.1 us
    ppermute x64, starting transfers between devices, to_x(): return lax.ppermute(v, 'tok', [(i, i ^ 2) for i in range(4)])  73.6 us
    dynamic_slice x10, local copies, waits for them, and re-layouts, swap_halves(): snd = lax.dynamic_slice_in_dim(w, (1 - core) * half, half, 1)  71.2 us
    concatenate x32, local copies, waits for them, and re-layouts, apply_rope(): jnp.concatenate([a * cos_t - b * sin_t, b * cos_t + a * sin_t], axis=-1)  65.9 us
    slice x2, local copies, waits for them, and re-layouts, device_fn(): gu_w = [swap_halves(w[l], f_half) for w in (w_gate, w_up)]  51.7 us
  transfers between devices with their start and end apart: 146, of which 62 were waited for; matrix products, arithmetic and copies ran while one was open for 43% of the time, Pallas kernels for 0%

profile of v1, /device:TPU:0, one launch (start us, length us, event | category | flops | bytes accessed | tf_op | source)
XLA Modules:
  0.0 2084.8 jit_solution(18037658745123428593)
XLA Ops:
  7.8 18.8 all-gather
  35.7 10.4 fusion.907
  75.5 8.5 fusion.906
  98.7 8.5 fusion.908
  121.8 9.5 fusion.909
  131.4 25.9 %fusion.904 = (bf16[1,1280,6912]{2,1,0:T(8,128)(2,1)}, bf16[1,1280,6912]{2,1,0:T(8,128)(2,1)}) fusion(bf16[2,1280,6912]{2,1,0:T(8,128)(2,1)} %param.19), kind=kLoop, calls=%fused_computation.1085 | loop fusion | bytes 70778880 | tf_op jit(solution)/shard_map/slice | solution.py:141
  157.2 25.8 %fusion.903 = (bf16[1,1280,6912]{2,1,0:T(8,128)(2,1)}, bf16[1,1280,6912]{2,1,0:T(8,128)(2,1)}) fusion(bf16[2,1280,6912]{2,1,0:T(8,128)(2,1)} %param.20), kind=kLoop, calls=%fused_computation.1084 | loop fusion | bytes 70778880 | tf_op jit(solution)/shard_map/slice | solution.py:141
  183.1 12.9 dynamic-slice_bitcast_fusion.6
  200.3 6.8 dynamic-slice_bitcast_fusion.4
  207.1 25.8 %fusion.905 = (bf16[1,6912,1280]{2,1,0:T(8,128)(2,1)}, bf16[1,6912,1280]{2,1,0:T(8,128)(2,1)}) fusion(bf16[2,6912,1280]{2,1,0:T(8,128)(2,1)} %param.21), kind=kLoop, calls=%fused_computation.1086 | loop fusion | bytes 70778880 | tf_op jit(solution)/shard_map/slice | solution.py:177
  237.0 11.7 collective-permute-done.3
  255.8 15.1 collective-permute-done.83
  312.0 17.4 collective-permute-done.10
  335.8 21.7 %collective-permute-done.12 = f32[256,1280]{1,0:T(8,128)} collective-permute-done((f32[256,1280]{1,0:T(8,128)}, f32[256,1280]{1,0:T(8,128)}, u32[]{:S(2)}, u32[]{:S(2)}) %collective-permute-start.12) | collective-permute-done | bytes 1310752 | tf_op jit(solution)/shard_map/ppermute | solution.py:51
  365.3 20.3 collective-permute-done.86
  426.8 14.9 collective-permute-done.8
  488.1 13.7 collective-permute-done.88
  501.8 12.5 collective-permute-done.13
  531.2 22.9 %collective-permute-done.91 = f32[256,1280]{1,0:T(8,128)S(1)} collective-permute-done((f32[256,1280]{1,0:T(8,128)S(1)}, f32[256,1280]{1,0:T(8,128)S(1)}, u32[]{:S(2)}, u32[]{:S(2)}) %collective-permute-start.91) | collective-permute-done | bytes 1310752 | tf_op jit(solution)/shard_map/ppermute | solution.py:60
  555.4 25.8 %collective-permute-done.16 = f32[256,1280]{1,0:T(8,128)} collective-permute-done((f32[256,1280]{1,0:T(8,128)}, f32[256,1280]{1,0:T(8,128)}, u32[]{:S(2)}, u32[]{:S(2)}) %collective-permute-start.16) | collective-permute-done | bytes 1310752 | tf_op jit(solution)/shard_map/ppermute | solution.py:60
  621.6 10.8 collective-permute-done.94
  706.6 14.8 collective-permute-done.33
  725.9 20.8 collective-permute-done.101
  751.2 20.8 collective-permute-done.107
  776.5 20.7 collective-permute-done.34
  801.8 46.1 %collective-permute-done.102 = f32[256,1152]{1,0:T(8,128)S(1)} collective-permute-done((f32[256,1152]{1,0:T(8,128)S(1)}, f32[256,1152]{1,0:T(8,128)S(1)}, u32[]{:S(2)}, u32[]{:S(2)}) %collective-permute-start.102) | collective-permute-done | bytes 1179680 | tf_op jit(solution)/shard_map/ppermute | solution.py:51
  852.9 20.2 collective-permute-done.96
  877.6 20.8 collective-permute-done.97
  906.1 17.6 collective-permute-done.22
  928.2 20.7 collective-permute-done.29
  953.4 20.8 collective-permute-done.24
  978.8 20.2 collective-permute-done.98
  1003.3 11.9 collective-permute-done.25
  1017.8 10.0 collective-permute-done.103
  1029.0 10.2 collective-permute-done.30
  1046.0 7.1 collective-permute-done.35
  1082.2 17.8 collective-permute-done.38
  1102.3 25.2 %collective-permute-done.111 = f32[256,1280]{1,0:T(8,128)} collective-permute-done((f32[256,1280]{1,0:T(8,128)}, f32[256,1280]{1,0:T(8,128)}, u32[]{:S(2)}, u32[]{:S(2)}) %collective-permute-start.111) | collective-permute-done | bytes 1310752 | tf_op jit(solution)/shard_map/ppermute | solution.py:60
  1160.5 15.0 collective-permute-done.41
  1230.7 35.1 %collective-permute-done.118 = f32[256,1280]{1,0:T(8,128)S(1)} collective-permute-done((f32[256,1280]{1,0:T(8,128)S(1)}, f32[256,1280]{1,0:T(8,128)S(1)}, u32[]{:S(2)}, u32[]{:S(2)}) %collective-permute-start.118) | collective-permute-done | bytes 1310752 | tf_op jit(solution)/shard_map/ppermute | solution.py:51
  1273.2 20.7 collective-permute-done.117
  1369.5 8.6 collective-permute-done.46
  1429.1 7.2 collective-permute-done.49
  1447.6 11.9 dynamic-slice_bitcast_fusion.2
  1462.6 11.6 collective-permute-done.122
  1476.7 25.2 %collective-permute-done.52 = f32[256,1280]{1,0:T(8,128)} collective-permute-done((f32[256,1280]{1,0:T(8,128)}, f32[256,1280]{1,0:T(8,128)}, u32[]{:S(2)}, u32[]{:S(2)}) %collective-permute-start.52) | collective-permute-done | bytes 1310752 | tf_op jit(solution)/shard_map/ppermute | solution.py:60
  1508.0 7.7 dynamic-slice_bitcast_fusion
  1525.0 27.1 %collective-permute-done.125 = bf16[2,2,64,1280]{3,2,1,0:T(8,128)(2,1)S(1)} collective-permute-done((bf16[2,2,64,1280]{3,2,1,0:T(8,128)(2,1)}, bf16[2,2,64,1280]{3,2,1,0:T(8,128)(2,1)S(1)}, u32[]{:S(2)}, u32[]{:S(2)}) %collective-permute-start.125) | collective-permute-done | bytes 655392 | tf_op jit(solution)/shard_map/ppermute | solution.py:60
  1635.8 37.6 %collective-permute-done.69 = f32[256,1152]{1,0:T(8,128)S(1)} collective-permute-done((f32[256,1152]{1,0:T(8,128)S(1)}, f32[256,1152]{1,0:T(8,128)S(1)}, u32[]{:S(2)}, u32[]{:S(2)}) %collective-permute-start.69) | collective-permute-done | bytes 1179680 | tf_op jit(solution)/shard_map/ppermute | solution.py:51
  1677.8 46.1 %collective-permute-done.64 = f32[256,1152]{1,0:T(8,128)S(1)} collective-permute-done((f32[256,1152]{1,0:T(8,128)S(1)}, f32[256,1152]{1,0:T(8,128)S(1)}, u32[]{:S(2)}, u32[]{:S(2)}) %collective-permute-start.64) | collective-permute-done | bytes 1179680 | tf_op jit(solution)/shard_map/ppermute | solution.py:51
  1736.7 12.5 collective-permute-done.60
  1753.9 71.2 %collective-permute-done.137 = f32[256,1152]{1,0:T(8,128)S(1)} collective-permute-done((f32[256,1152]{1,0:T(8,128)S(1)}, f32[256,1152]{1,0:T(8,128)S(1)}, u32[]{:S(2)}, u32[]{:S(2)}) %collective-permute-start.137) | collective-permute-done | bytes 1179680 | tf_op jit(solution)/shard_map/ppermute | solution.py:51
  1836.3 39.3 %collective-permute-done.132 = f32[256,1152]{1,0:T(8,128)S(1)} collective-permute-done((f32[256,1152]{1,0:T(8,128)S(1)}, f32[256,1152]{1,0:T(8,128)S(1)}, u32[]{:S(2)}, u32[]{:S(2)}) %collective-permute-start.132) | collective-permute-done | bytes 1179680 | tf_op jit(solution)/shard_map/ppermute | solution.py:51
  1883.9 17.0 collective-permute-done.128
  1904.1 9.5 collective-permute-done.71
  1917.2 9.0 collective-permute-done.66
  1928.8 10.1 collective-permute-done.61
  1938.9 11.6 collective-permute-done.139
  1957.5 7.5 collective-permute-done.134
  1969.3 12.6 collective-permute-done.129
  2003.6 18.4 collective-permute-done.74
  2023.5 26.1 %collective-permute-done.142 = f32[256,1280]{1,0:T(8,128)S(1)} collective-permute-done((f32[256,1280]{1,0:T(8,128)S(1)}, f32[256,1280]{1,0:T(8,128)S(1)}, u32[]{:S(2)}, u32[]{:S(2)}) %collective-permute-start.142) | collective-permute-done | bytes 1310752 | tf_op jit(solution)/shard_map/ppermute | solution.py:60
  2055.3 13.2 collective-permute-done.144
  2068.6 13.9 collective-permute-done.76
  (1022 shorter events, 888.9 us)
Async XLA Ops:
  1.5 231.9 %collective-permute-start.2 = (bf16[64,1280]{1,0:T(8,128)(2,1)S(1)}, bf16[64,1280]{1,0:T(8,128)(2,1)S(1)}, u32[]{:S(2)}, u32[]{:S(2)}) collective-permute-start(bf16[64,1280]{1,0:T(8,128)(2,1)S(1)} %get-tuple-element.100), channel_id=1, source_target_pairs={{0,3},{1,2},{2,1},{3,0},{4,7},{5,6},{6,5},{7,4}} | collective-permute-start | bytes 491528 | tf_op jit(solution)/shard_map/ppermute | solution.py:57
  4.3 229.6 %collective-permute-start.1 = (bf16[64,1280]{1,0:T(8,128)(2,1)S(1)}, bf16[64,1280]{1,0:T(8,128)(2,1)S(1)}, u32[]{:S(2)}, u32[]{:S(2)}) collective-permute-start(bf16[64,1280]{1,0:T(8,128)(2,1)S(1)} %get-tuple-element.101), channel_id=1, source_target_pairs={{0,2},{1,3},{2,0},{3,1},{4,6},{5,7},{6,4},{7,5}} | collective-permute-start | bytes 491528 | tf_op jit(solution)/shard_map/ppermute | solution.py:51
  4.9 228.3 %collective-permute-start = (bf16[64,1280]{1,0:T(8,128)(2,1)S(1)}, bf16[64,1280]{1,0:T(8,128)(2,1)S(1)}, u32[]{:S(2)}, u32[]{:S(2)}) collective-permute-start(bf16[64,1280]{1,0:T(8,128)(2,1)S(1)} %get-tuple-element.102), channel_id=1, source_target_pairs={{0,1},{1,0},{2,3},{3,2},{4,5},{5,4},{6,7},{7,6}} | collective-permute-start | bytes 491528 | tf_op jit(solution)/shard_map/ppermute | solution.py:54
  5.7 230.5 %collective-permute-start.80 = (bf16[64,1280]{1,0:T(8,128)(2,1)S(1)}, bf16[64,1280]{1,0:T(8,128)(2,1)S(1)}, u32[]{:S(2)}, u32[]{:S(2)}) collective-permute-start(bf16[64,1280]{1,0:T(8,128)(2,1)S(1)} %get-tuple-element.120), channel_id=1, source_target_pairs={{0,3},{1,2},{2,1},{3,0},{4,7},{5,6},{6,5},{7,4}} | collective-permute-start | bytes 491528 | tf_op jit(solution)/shard_map/ppermute | solution.py:57
  7.1 229.1 %collective-permute-start.79 = (bf16[64,1280]{1,0:T(8,128)(2,1)S(1)}, bf16[64,1280]{1,0:T(8,128)(2,1)S(1)}, u32[]{:S(2)}, u32[]{:S(2)}) collective-permute-start(bf16[64,1280]{1,0:T(8,128)(2,1)S(1)} %get-tuple-element.121), channel_id=1, source_target_pairs={{0,2},{1,3},{2,0},{3,1},{4,6},{5,7},{6,4},{7,5}} | collective-permute-start | bytes 491528 | tf_op jit(solution)/shard_map/ppermute | solution.py:51
  233.4 62.4 %collective-permute-start.9 = (bf16[1280,10,128]{0,2,1:T(8,128)(2,1)}, bf16[1280,10,128]{0,2,1:T(8,128)(2,1)S(1)}, u32[]{:S(2)}, u32[]{:S(2)}) collective-permute-start(bf16[1280,10,128]{0,2,1:T(8,128)(2,1)} %bitcast.871), channel_id=1, source_target_pairs={{0,1},{1,0},{2,3},{3,2},{4,5},{5,4},{6,7},{7,6}} | collective-permute-start | bytes 9830408 | tf_op jit(solution)/shard_map/ppermute | solution.py:54
  233.9 63.8 %collective-permute-start.11 = (bf16[1280,10,128]{0,2,1:T(8,128)(2,1)}, bf16[1280,10,128]{0,2,1:T(8,128)(2,1)S(1)}, u32[]{:S(2)}, u32[]{:S(2)}) collective-permute-start(bf16[1280,10,128]{0,2,1:T(8,128)(2,1)} %bitcast.872), channel_id=1, source_target_pairs={{0,1},{1,0},{2,3},{3,2},{4,5},{5,4},{6,7},{7,6}} | collective-permute-start | bytes 9830408 | tf_op jit(solution)/shard_map/ppermute | solution.py:54
  235.6 70.6 %collective-permute-start.7 = (bf16[1280,10,128]{0,2,1:T(8,128)(2,1)S(1)}, bf16[1280,10,128]{0,2,1:T(8,128)(2,1)S(1)}, u32[]{:S(2)}, u32[]{:S(2)}) collective-permute-start(bf16[1280,10,128]{0,2,1:T(8,128)(2,1)S(1)} %bitcast.870), channel_id=1, source_target_pairs={{0,1},{1,0},{2,3},{3,2},{4,5},{5,4},{6,7},{7,6}} | collective-permute-start | bytes 9830408 | tf_op jit(solution)/shard_map/ppermute | solution.py:54
  295.7 915.7 %collective-permute-start.45 = (bf16[1280,10,128]{0,2,1:T(8,128)(2,1)}, bf16[1280,10,128]{0,2,1:T(8,128)(2,1)}, u32[]{:S(2)}, u32[]{:S(2)}) collective-permute-start(bf16[1280,10,128]{0,2,1:T(8,128)(2,1)} %bitcast.78), channel_id=1, source_target_pairs={{0,1},{1,0},{2,3},{3,2},{4,5},{5,4},{6,7},{7,6}} | collective-permute-start | bytes 9830408 | tf_op jit(solution)/shard_map/ppermute | solution.py:54
  295.7 368.6 %collective-permute-start.21 = (bf16[1280,3456]{1,0:T(8,128)(2,1)}, bf16[1280,3456]{1,0:T(8,128)(2,1)}, u32[]{:S(2)}, u32[]{:S(2)}) collective-permute-start(bf16[1280,3456]{1,0:T(8,128)(2,1)} %get-tuple-element.21), channel_id=1, source_target_pairs={{0,1},{1,0},{2,3},{3,2},{4,5},{5,4},{6,7},{7,6}} | collective-permute-start | bytes 26542088 | tf_op jit(solution)/shard_map/ppermute | solution.py:54
  301.4 56.1 %collective-permute-start.12 = (f32[256,1280]{1,0:T(8,128)}, f32[256,1280]{1,0:T(8,128)}, u32[]{:S(2)}, u32[]{:S(2)}) collective-permute-start(f32[256,1280]{1,0:T(8,128)} %convolution_add_fusion.74), channel_id=1, source_target_pairs={{0,2},{1,3},{2,0},{3,1},{4,6},{5,7},{6,4},{7,5}} | collective-permute-start | bytes 3932168 | tf_op jit(solution)/shard_map/ppermute | solution.py:51
  306.2 79.3 %collective-permute-start.86 = (f32[256,1280]{1,0:T(8,128)}, f32[256,1280]{1,0:T(8,128)}, u32[]{:S(2)}, u32[]{:S(2)}) collective-permute-start(f32[256,1280]{1,0:T(8,128)} %convolution_add_fusion.60), channel_id=1, source_target_pairs={{0,2},{1,3},{2,0},{3,1},{4,6},{5,7},{6,4},{7,5}} | collective-permute-start | bytes 3932168 | tf_op jit(solution)/shard_map/ppermute | solution.py:51
  329.4 84.3 %collective-permute-start.87 = (f32[256,1280]{1,0:T(8,128)}, f32[256,1280]{1,0:T(8,128)}, u32[]{:S(2)}, u32[]{:S(2)}) collective-permute-start(f32[256,1280]{1,0:T(8,128)} %convolution_add_fusion.58), channel_id=1, source_target_pairs={{0,2},{1,3},{2,0},{3,1},{4,6},{5,7},{6,4},{7,5}} | collective-permute-start | bytes 3932168 | tf_op jit(solution)/shard_map/ppermute | solution.py:51
  357.5 326.6 %collective-permute-start.23 = (bf16[1280,3456]{1,0:T(8,128)(2,1)}, bf16[1280,3456]{1,0:T(8,128)(2,1)}, u32[]{:S(2)}, u32[]{:S(2)}) collective-permute-start(bf16[1280,3456]{1,0:T(8,128)(2,1)} %get-tuple-element.19), channel_id=1, source_target_pairs={{0,1},{1,0},{2,3},{3,2},{4,5},{5,4},{6,7},{7,6}} | collective-permute-start | bytes 26542088 | tf_op jit(solution)/shard_map/ppermute | solution.py:54
  385.6 56.2 %collective-permute-start.8 = (f32[256,1280]{1,0:T(8,128)}, f32[256,1280]{1,0:T(8,128)}, u32[]{:S(2)}, u32[]{:S(2)}) collective-permute-start(f32[256,1280]{1,0:T(8,128)} %convolution_add_fusion.78), channel_id=1, source_target_pairs={{0,2},{1,3},{2,0},{3,1},{4,6},{5,7},{6,4},{7,5}} | collective-permute-start | bytes 3932168 | tf_op jit(solution)/shard_map/ppermute | solution.py:51
  413.7 60.6 %collective-permute-start.85 = (f32[256,1280]{1,0:T(8,128)}, f32[256,1280]{1,0:T(8,128)}, u32[]{:S(2)}, u32[]{:S(2)}) collective-permute-start(f32[256,1280]{1,0:T(8,128)} %convolution_add_fusion.62), channel_id=1, source_target_pairs={{0,2},{1,3},{2,0},{3,1},{4,6},{5,7},{6,4},{7,5}} | collective-permute-start | bytes 3932168 | tf_op jit(solution)/shard_map/ppermute | solution.py:51
  526.8 54.4 %collective-permute-start.16 = (f32[256,1280]{1,0:T(8,128)}, f32[256,1280]{1,0:T(8,128)}, u32[]{:S(2)}, u32[]{:S(2)}) collective-permute-start(f32[256,1280]{1,0:T(8,128)} %convolution_add_fusion.72), channel_id=1, source_target_pairs={{0,4},{4,0},{1,5},{5,1},{2,6},{6,2},{3,7},{7,3}} | collective-permute-start | bytes 3932168 | tf_op jit(solution)/shard_map/ppermute | solution.py:60
  664.3 542.3 %collective-permute-start.47 = (bf16[1280,10,128]{0,2,1:T(8,128)(2,1)}, bf16[1280,10,128]{0,2,1:T(8,128)(2,1)}, u32[]{:S(2)}, u32[]{:S(2)}) collective-permute-start(bf16[1280,10,128]{0,2,1:T(8,128)(2,1)} %bitcast.84), channel_id=1, source_target_pairs={{0,1},{1,0},{2,3},{3,2},{4,5},{5,4},{6,7},{7,6}} | collective-permute-start | bytes 9830408 | tf_op jit(solution)/shard_map/ppermute | solution.py:54
  671.7 49.7 %collective-permute-start.33 = (f32[256,1152]{1,0:T(8,128)S(1)}, f32[256,1152]{1,0:T(8,128)S(1)}, u32[]{:S(2)}, u32[]{:S(2)}) collective-permute-start(f32[256,1152]{1,0:T(8,128)S(1)} %convolution_add_fusion.38), channel_id=1, source_target_pairs={{0,2},{1,3},{2,0},{3,1},{4,6},{5,7},{6,4},{7,5}} | collective-permute-start | bytes 3538952 | tf_op jit(solution)/shard_map/ppermute | solution.py:51
  684.1 62.6 %collective-permute-start.101 = (f32[256,1152]{1,0:T(8,128)S(1)}, f32[256,1152]{1,0:T(8,128)S(1)}, u32[]{:S(2)}, u32[]{:S(2)}) collective-permute-start(f32[256,1152]{1,0:T(8,128)S(1)} %convolution_add_fusion.18), channel_id=1, source_target_pairs={{0,2},{1,3},{2,0},{3,1},{4,6},{5,7},{6,4},{7,5}} | collective-permute-start | bytes 3538952 | tf_op jit(solution)/shard_map/ppermute | solution.py:51
  703.1 68.9 %collective-permute-start.107 = (f32[256,1152]{1,0:T(8,128)S(1)}, f32[256,1152]{1,0:T(8,128)S(1)}, u32[]{:S(2)}, u32[]{:S(2)}) collective-permute-start(f32[256,1152]{1,0:T(8,128)S(1)} %convolution_add_fusion.12), channel_id=1, source_target_pairs={{0,2},{1,3},{2,0},{3,1},{4,6},{5,7},{6,4},{7,5}} | collective-permute-start | bytes 3538952 | tf_op jit(solution)/shard_map/ppermute | solution.py:51
  721.4 75.8 %collective-permute-start.34 = (f32[256,1152]{1,0:T(8,128)S(1)}, f32[256,1152]{1,0:T(8,128)S(1)}, u32[]{:S(2)}, u32[]{:S(2)}) collective-permute-start(f32[256,1152]{1,0:T(8,128)S(1)} %convolution_add_fusion.36), channel_id=1, source_target_pairs={{0,2},{1,3},{2,0},{3,1},{4,6},{5,7},{6,4},{7,5}} | collective-permute-start | bytes 3538952 | tf_op jit(solution)/shard_map/ppermute | solution.py:51
  746.7 154.7 %collective-permute-start.28 = (f32[256,1152]{1,0:T(8,128)S(1)}, f32[256,1152]{1,0:T(8,128)S(1)}, u32[]{:S(2)}, u32[]{:S(2)}) collective-permute-start(f32[256,1152]{1,0:T(8,128)S(1)} %convolution_add_fusion.42), channel_id=1, source_target_pairs={{0,2},{1,3},{2,0},{3,1},{4,6},{5,7},{6,4},{7,5}} | collective-permute-start | bytes 3538952 | tf_op jit(solution)/shard_map/ppermute | solution.py:51
  772.0 75.8 %collective-permute-start.102 = (f32[256,1152]{1,0:T(8,128)S(1)}, f32[256,1152]{1,0:T(8,128)S(1)}, u32[]{:S(2)}, u32[]{:S(2)}) collective-permute-start(f32[256,1152]{1,0:T(8,128)S(1)} %convolution_add_fusion.16), channel_id=1, source_target_pairs={{0,2},{1,3},{2,0},{3,1},{4,6},{5,7},{6,4},{7,5}} | collective-permute-start | bytes 3538952 | tf_op jit(solution)/shard_map/ppermute | solution.py:51
  797.3 75.8 %collective-permute-start.96 = (f32[256,1152]{1,0:T(8,128)S(1)}, f32[256,1152]{1,0:T(8,128)S(1)}, u32[]{:S(2)}, u32[]{:S(2)}) collective-permute-start(f32[256,1152]{1,0:T(8,128)S(1)} %convolution_add_fusion.22), channel_id=1, source_target_pairs={{0,2},{1,3},{2,0},{3,1},{4,6},{5,7},{6,4},{7,5}} | collective-permute-start | bytes 3538952 | tf_op jit(solution)/shard_map/ppermute | solution.py:51
  847.8 50.6 %collective-permute-start.97 = (f32[256,1152]{1,0:T(8,128)S(1)}, f32[256,1152]{1,0:T(8,128)S(1)}, u32[]{:S(2)}, u32[]{:S(2)}) collective-permute-start(f32[256,1152]{1,0:T(8,128)S(1)} %convolution_add_fusion.20), channel_id=1, source_target_pairs={{0,2},{1,3},{2,0},{3,1},{4,6},{5,7},{6,4},{7,5}} | collective-permute-start | bytes 3538952 | tf_op jit(solution)/shard_map/ppermute | solution.py:51
  873.1 50.6 %collective-permute-start.22 = (f32[256,1152]{1,0:T(8,128)S(1)}, f32[256,1152]{1,0:T(8,128)S(1)}, u32[]{:S(2)}, u32[]{:S(2)}) collective-permute-start(f32[256,1152]{1,0:T(8,128)S(1)} %convolution_add_fusion.46), channel_id=1, source_target_pairs={{0,2},{1,3},{2,0},{3,1},{4,6},{5,7},{6,4},{7,5}} | collective-permute-start | bytes 3538952 | tf_op jit(solution)/shard_map/ppermute | solution.py:51
  898.4 303.1 %collective-permute-start.43 = (bf16[1280,10,128]{0,2,1:T(8,128)(2,1)}, bf16[1280,10,128]{0,2,1:T(8,128)(2,1)}, u32[]{:S(2)}, u32[]{:S(2)}) collective-permute-start(bf16[1280,10,128]{0,2,1:T(8,128)(2,1)} %bitcast.71), channel_id=1, source_target_pairs={{0,1},{1,0},{2,3},{3,2},{4,5},{5,4},{6,7},{7,6}} | collective-permute-start | bytes 9830408 | tf_op jit(solution)/shard_map/ppermute | solution.py:54
  901.4 47.5 %collective-permute-start.29 = (f32[256,1152]{1,0:T(8,128)S(1)}, f32[256,1152]{1,0:T(8,128)S(1)}, u32[]{:S(2)}, u32[]{:S(2)}) collective-permute-start(f32[256,1152]{1,0:T(8,128)S(1)} %convolution_add_fusion.40), channel_id=1, source_target_pairs={{0,2},{1,3},{2,0},{3,1},{4,6},{5,7},{6,4},{7,5}} | collective-permute-start | bytes 3538952 | tf_op jit(solution)/shard_map/ppermute | solution.py:51
  923.7 50.6 %collective-permute-start.24 = (f32[256,1152]{1,0:T(8,128)S(1)}, f32[256,1152]{1,0:T(8,128)S(1)}, u32[]{:S(2)}, u32[]{:S(2)}) collective-permute-start(f32[256,1152]{1,0:T(8,128)S(1)} %convolution_add_fusion.44), channel_id=1, source_target_pairs={{0,2},{1,3},{2,0},{3,1},{4,6},{5,7},{6,4},{7,5}} | collective-permute-start | bytes 3538952 | tf_op jit(solution)/shard_map/ppermute | solution.py:51
  948.9 53.8 %collective-permute-start.108 = (bf16[256,1152]{1,0:T(8,128)(2,1)S(1)}, bf16[256,1152]{1,0:T(8,128)(2,1)S(1)}, u32[]{:S(2)}, u32[]{:S(2)}) collective-permute-start(bf16[256,1152]{1,0:T(8,128)(2,1)S(1)} %multiply_convert_fusion.16), channel_id=1, source_target_pairs={{0,2},{1,3},{2,0},{3,1},{4,6},{5,7},{6,4},{7,5}} | collective-permute-start | bytes 1769480 | tf_op jit(solution)/shard_map/ppermute | solution.py:51
  1076.0 51.5 %collective-permute-start.111 = (f32[256,1280]{1,0:T(8,128)}, f32[256,1280]{1,0:T(8,128)}, u32[]{:S(2)}, u32[]{:S(2)}) collective-permute-start(f32[256,1280]{1,0:T(8,128)} %fusion.121), channel_id=1, source_target_pairs={{0,4},{4,0},{1,5},{5,1},{2,6},{6,2},{3,7},{7,3}} | collective-permute-start | bytes 3932168 | tf_op jit(solution)/shard_map/ppermute | solution.py:60
  1206.1 109.0 %collective-permute-start.116 = (f32[256,1280]{1,0:T(8,128)}, f32[256,1280]{1,0:T(8,128)}, u32[]{:S(2)}, u32[]{:S(2)}) collective-permute-start(f32[256,1280]{1,0:T(8,128)} %convolution_add_fusion.54), channel_id=1, source_target_pairs={{0,2},{1,3},{2,0},{3,1},{4,6},{5,7},{6,4},{7,5}} | collective-permute-start | bytes 3932168 | tf_op jit(solution)/shard_map/ppermute | solution.py:51
  1209.8 56.0 %collective-permute-start.118 = (f32[256,1280]{1,0:T(8,128)S(1)}, f32[256,1280]{1,0:T(8,128)S(1)}, u32[]{:S(2)}, u32[]{:S(2)}) collective-permute-start(f32[256,1280]{1,0:T(8,128)S(1)} %convolution_add_fusion.50), channel_id=1, source_target_pairs={{0,2},{1,3},{2,0},{3,1},{4,6},{5,7},{6,4},{7,5}} | collective-permute-start | bytes 3932168 | tf_op jit(solution)/shard_map/ppermute | solution.py:51
  1215.4 78.5 %collective-permute-start.117 = (f32[256,1280]{1,0:T(8,128)}, f32[256,1280]{1,0:T(8,128)}, u32[]{:S(2)}, u32[]{:S(2)}) collective-permute-start(f32[256,1280]{1,0:T(8,128)} %convolution_add_fusion.52), channel_id=1, source_target_pairs={{0,2},{1,3},{2,0},{3,1},{4,6},{5,7},{6,4},{7,5}} | collective-permute-start | bytes 3932168 | tf_op jit(solution)/shard_map/ppermute | solution.py:51
  1220.5 130.1 %collective-permute-start.44 = (f32[256,1280]{1,0:T(8,128)}, f32[256,1280]{1,0:T(8,128)}, u32[]{:S(2)}, u32[]{:S(2)}) collective-permute-start(f32[256,1280]{1,0:T(8,128)} %convolution_add_fusion.70), channel_id=1, source_target_pairs={{0,2},{1,3},{2,0},{3,1},{4,6},{5,7},{6,4},{7,5}} | collective-permute-start | bytes 3932168 | tf_op jit(solution)/shard_map/ppermute | solution.py:51
  1226.1 133.7 %collective-permute-start.48 = (f32[256,1280]{1,0:T(8,128)}, f32[256,1280]{1,0:T(8,128)}, u32[]{:S(2)}, u32[]{:S(2)}) collective-permute-start(f32[256,1280]{1,0:T(8,128)} %convolution_add_fusion.66), channel_id=1, source_target_pairs={{0,2},{1,3},{2,0},{3,1},{4,6},{5,7},{6,4},{7,5}} | collective-permute-start | bytes 3932168 | tf_op jit(solution)/shard_map/ppermute | solution.py:51
  1265.8 112.4 %collective-permute-start.46 = (f32[256,1280]{1,0:T(8,128)}, f32[256,1280]{1,0:T(8,128)}, u32[]{:S(2)}, u32[]{:S(2)}) collective-permute-start(f32[256,1280]{1,0:T(8,128)} %convolution_add_fusion.68), channel_id=1, source_target_pairs={{0,2},{1,3},{2,0},{3,1},{4,6},{5,7},{6,4},{7,5}} | collective-permute-start | bytes 3932168 | tf_op jit(solution)/shard_map/ppermute | solution.py:51
  1350.1 86.3 %collective-permute-start.120 = (bf16[256,1280]{1,0:T(8,128)(2,1)}, bf16[256,1280]{1,0:T(8,128)(2,1)}, u32[]{:S(2)}, u32[]{:S(2)}) collective-permute-start(bf16[256,1280]{1,0:T(8,128)(2,1)} %bitcast.182), channel_id=1, source_target_pairs={{0,1},{1,0},{2,3},{3,2},{4,5},{5,4},{6,7},{7,6}} | collective-permute-start | bytes 1966088 | tf_op jit(solution)/shard_map/ppermute | solution.py:54
  1350.1 74.3 %collective-permute-start.119 = (bf16[256,1280]{1,0:T(8,128)(2,1)}, bf16[256,1280]{1,0:T(8,128)(2,1)}, u32[]{:S(2)}, u32[]{:S(2)}) collective-permute-start(bf16[256,1280]{1,0:T(8,128)(2,1)} %bitcast.182), channel_id=1, source_target_pairs={{0,2},{1,3},{2,0},{3,1},{4,6},{5,7},{6,4},{7,5}} | collective-permute-start | bytes 1966088 | tf_op jit(solution)/shard_map/ppermute | solution.py:51
  1446.1 55.8 %collective-permute-start.52 = (f32[256,1280]{1,0:T(8,128)}, f32[256,1280]{1,0:T(8,128)}, u32[]{:S(2)}, u32[]{:S(2)}) collective-permute-start(f32[256,1280]{1,0:T(8,128)} %convolution_add_fusion.64), channel_id=1, source_target_pairs={{0,4},{4,0},{1,5},{5,1},{2,6},{6,2},{3,7},{7,3}} | collective-permute-start | bytes 3932168 | tf_op jit(solution)/shard_map/ppermute | solution.py:60
  1459.5 131.6 %collective-permute-start.57 = (bf16[1280,3456]{1,0:T(8,128)(2,1)}, bf16[1280,3456]{1,0:T(8,128)(2,1)}, u32[]{:S(2)}, u32[]{:S(2)}) collective-permute-start(bf16[1280,3456]{1,0:T(8,128)(2,1)} %get-tuple-element.17), channel_id=1, source_target_pairs={{0,1},{1,0},{2,3},{3,2},{4,5},{5,4},{6,7},{7,6}} | collective-permute-start | bytes 26542088 | tf_op jit(solution)/shard_map/ppermute | solution.py:54
  1515.7 79.8 %collective-permute-start.59 = (bf16[1280,3456]{1,0:T(8,128)(2,1)S(1)}, bf16[1280,3456]{1,0:T(8,128)(2,1)}, u32[]{:S(2)}, u32[]{:S(2)}) collective-permute-start(bf16[1280,3456]{1,0:T(8,128)(2,1)S(1)} %get-tuple-element.15), channel_id=1, source_target_pairs={{0,1},{1,0},{2,3},{3,2},{4,5},{5,4},{6,7},{7,6}} | collective-permute-start | bytes 26542088 | tf_op jit(solution)/shard_map/ppermute | solution.py:54
  1552.8 38.3 %collective-permute-start.56 = (bf16[2,256,1280]{2,1,0:T(8,128)(2,1)S(1)}, bf16[2,256,1280]{2,1,0:T(8,128)(2,1)S(1)}, u32[]{:S(2)}, u32[]{:S(2)}) collective-permute-start(bf16[2,256,1280]{2,1,0:T(8,128)(2,1)S(1)} %bitcast.924), channel_id=1, source_target_pairs={{0,1},{1,0},{2,3},{3,2},{4,5},{5,4},{6,7},{7,6}} | collective-permute-start | bytes 3932168 | tf_op jit(solution)/shard_map/ppermute | solution.py:54
  1552.8 60.3 %collective-permute-start.126 = (bf16[2,256,1280]{2,1,0:T(8,128)(2,1)S(1)}, bf16[2,256,1280]{2,1,0:T(8,128)(2,1)S(1)}, u32[]{:S(2)}, u32[]{:S(2)}) collective-permute-start(bf16[2,256,1280]{2,1,0:T(8,128)(2,1)S(1)} %bitcast.919), channel_id=1, source_target_pairs={{0,1},{1,0},{2,3},{3,2},{4,5},{5,4},{6,7},{7,6}} | collective-permute-start | bytes 3932168 | tf_op jit(solution)/shard_map/ppermute | solution.py:54
  1594.0 38.3 %collective-permute-start.58 = (f32[256,1152]{1,0:T(8,128)S(1)}, f32[256,1152]{1,0:T(8,128)S(1)}, u32[]{:S(2)}, u32[]{:S(2)}) collective-permute-start(f32[256,1152]{1,0:T(8,128)S(1)} %convolution_add_fusion.34), channel_id=1, source_target_pairs={{0,2},{1,3},{2,0},{3,1},{4,6},{5,7},{6,4},{7,5}} | collective-permute-start | bytes 3538952 | tf_op jit(solution)/shard_map/ppermute | solution.py:51
  1598.4 130.0 %collective-permute-start.70 = (f32[256,1152]{1,0:T(8,128)S(1)}, f32[256,1152]{1,0:T(8,128)S(1)}, u32[]{:S(2)}, u32[]{:S(2)}) collective-permute-start(f32[256,1152]{1,0:T(8,128)S(1)} %convolution_add_fusion.24), channel_id=1, source_target_pairs={{0,2},{1,3},{2,0},{3,1},{4,6},{5,7},{6,4},{7,5}} | collective-permute-start | bytes 3538952 | tf_op jit(solution)/shard_map/ppermute | solution.py:51
  1602.3 71.2 %collective-permute-start.69 = (f32[256,1152]{1,0:T(8,128)S(1)}, f32[256,1152]{1,0:T(8,128)S(1)}, u32[]{:S(2)}, u32[]{:S(2)}) collective-permute-start(f32[256,1152]{1,0:T(8,128)S(1)} %convolution_add_fusion.26), channel_id=1, source_target_pairs={{0,2},{1,3},{2,0},{3,1},{4,6},{5,7},{6,4},{7,5}} | collective-permute-start | bytes 3538952 | tf_op jit(solution)/shard_map/ppermute | solution.py:51
  1606.7 125.4 %collective-permute-start.65 = (f32[256,1152]{1,0:T(8,128)S(1)}, f32[256,1152]{1,0:T(8,128)S(1)}, u32[]{:S(2)}, u32[]{:S(2)}) collective-permute-start(f32[256,1152]{1,0:T(8,128)S(1)} %convolution_add_fusion.28), channel_id=1, source_target_pairs={{0,2},{1,3},{2,0},{3,1},{4,6},{5,7},{6,4},{7,5}} | collective-permute-start | bytes 3538952 | tf_op jit(solution)/shard_map/ppermute | solution.py:51
  1613.1 110.8 %collective-permute-start.64 = (f32[256,1152]{1,0:T(8,128)S(1)}, f32[256,1152]{1,0:T(8,128)S(1)}, u32[]{:S(2)}, u32[]{:S(2)}) collective-permute-start(f32[256,1152]{1,0:T(8,128)S(1)} %convolution_add_fusion.30), channel_id=1, source_target_pairs={{0,2},{1,3},{2,0},{3,1},{4,6},{5,7},{6,4},{7,5}} | collective-permute-start | bytes 3538952 | tf_op jit(solution)/shard_map/ppermute | solution.py:51
  1632.3 117.0 %collective-permute-start.60 = (f32[256,1152]{1,0:T(8,128)S(1)}, f32[256,1152]{1,0:T(8,128)S(1)}, u32[]{:S(2)}, u32[]{:S(2)}) collective-permute-start(f32[256,1152]{1,0:T(8,128)S(1)} %convolution_add_fusion.32), channel_id=1, source_target_pairs={{0,2},{1,3},{2,0},{3,1},{4,6},{5,7},{6,4},{7,5}} | collective-permute-start | bytes 3538952 | tf_op jit(solution)/shard_map/ppermute | solution.py:51
  1673.4 159.2 %collective-permute-start.127 = (f32[256,1152]{1,0:T(8,128)S(1)}, f32[256,1152]{1,0:T(8,128)S(1)}, u32[]{:S(2)}, u32[]{:S(2)}) collective-permute-start(f32[256,1152]{1,0:T(8,128)S(1)} %convolution_add_fusion.10), channel_id=1, source_target_pairs={{0,2},{1,3},{2,0},{3,1},{4,6},{5,7},{6,4},{7,5}} | collective-permute-start | bytes 3538952 | tf_op jit(solution)/shard_map/ppermute | solution.py:51
  1724.0 105.6 %collective-permute-start.138 = (f32[256,1152]{1,0:T(8,128)S(1)}, f32[256,1152]{1,0:T(8,128)S(1)}, u32[]{:S(2)}, u32[]{:S(2)}) collective-permute-start(f32[256,1152]{1,0:T(8,128)S(1)} %convolution_add_fusion), channel_id=1, source_target_pairs={{0,2},{1,3},{2,0},{3,1},{4,6},{5,7},{6,4},{7,5}} | collective-permute-start | bytes 3538952 | tf_op jit(solution)/shard_map/ppermute | solution.py:51
  1728.4 96.7 %collective-permute-start.137 = (f32[256,1152]{1,0:T(8,128)S(1)}, f32[256,1152]{1,0:T(8,128)S(1)}, u32[]{:S(2)}, u32[]{:S(2)}) collective-permute-start(f32[256,1152]{1,0:T(8,128)S(1)} %convolution_add_fusion.2), channel_id=1, source_target_pairs={{0,2},{1,3},{2,0},{3,1},{4,6},{5,7},{6,4},{7,5}} | collective-permute-start | bytes 3538952 | tf_op jit(solution)/shard_map/ppermute | solution.py:51
  1732.0 146.7 %collective-permute-start.133 = (f32[256,1152]{1,0:T(8,128)S(1)}, f32[256,1152]{1,0:T(8,128)S(1)}, u32[]{:S(2)}, u32[]{:S(2)}) collective-permute-start(f32[256,1152]{1,0:T(8,128)S(1)} %convolution_add_fusion.4), channel_id=1, source_target_pairs={{0,2},{1,3},{2,0},{3,1},{4,6},{5,7},{6,4},{7,5}} | collective-permute-start | bytes 3538952 | tf_op jit(solution)/shard_map/ppermute | solution.py:51
  1749.3 126.4 %collective-permute-start.132 = (f32[256,1152]{1,0:T(8,128)S(1)}, f32[256,1152]{1,0:T(8,128)S(1)}, u32[]{:S(2)}, u32[]{:S(2)}) collective-permute-start(f32[256,1152]{1,0:T(8,128)S(1)} %convolution_add_fusion.6), channel_id=1, source_target_pairs={{0,2},{1,3},{2,0},{3,1},{4,6},{5,7},{6,4},{7,5}} | collective-permute-start | bytes 3538952 | tf_op jit(solution)/shard_map/ppermute | solution.py:51
  1825.1 75.8 %collective-permute-start.128 = (f32[256,1152]{1,0:T(8,128)S(1)}, f32[256,1152]{1,0:T(8,128)S(1)}, u32[]{:S(2)}, u32[]{:S(2)}) collective-permute-start(f32[256,1152]{1,0:T(8,128)S(1)} %convolution_add_fusion.8), channel_id=1, source_target_pairs={{0,2},{1,3},{2,0},{3,1},{4,6},{5,7},{6,4},{7,5}} | collective-permute-start | bytes 3538952 | tf_op jit(solution)/shard_map/ppermute | solution.py:51
  1829.5 136.5 %collective-permute-start.72 = (bf16[256,1152]{1,0:T(8,128)(2,1)S(1)}, bf16[256,1152]{1,0:T(8,128)(2,1)S(1)}, u32[]{:S(2)}, u32[]{:S(2)}) collective-permute-start(bf16[256,1152]{1,0:T(8,128)(2,1)S(1)} %multiply_convert_fusion.19), channel_id=1, source_target_pairs={{0,1},{1,0},{2,3},{3,2},{4,5},{5,4},{6,7},{7,6}} | collective-permute-start | bytes 1769480 | tf_op jit(solution)/shard_map/ppermute | solution.py:54
  1832.6 80.9 %collective-permute-start.71 = (bf16[256,1152]{1,0:T(8,128)(2,1)S(1)}, bf16[256,1152]{1,0:T(8,128)(2,1)S(1)}, u32[]{:S(2)}, u32[]{:S(2)}) collective-permute-start(bf16[256,1152]{1,0:T(8,128)(2,1)S(1)} %multiply_convert_fusion.19), channel_id=1, source_target_pairs={{0,2},{1,3},{2,0},{3,1},{4,6},{5,7},{6,4},{7,5}} | collective-permute-start | bytes 1769480 | tf_op jit(solution)/shard_map/ppermute | solution.py:51
  1875.7 91.0 %collective-permute-start.67 = (bf16[256,1152]{1,0:T(8,128)(2,1)S(1)}, bf16[256,1152]{1,0:T(8,128)(2,1)S(1)}, u32[]{:S(2)}, u32[]{:S(2)}) collective-permute-start(bf16[256,1152]{1,0:T(8,128)(2,1)S(1)} %multiply_convert_fusion.20), channel_id=1, source_target_pairs={{0,1},{1,0},{2,3},{3,2},{4,5},{5,4},{6,7},{7,6}} | collective-permute-start | bytes 1769480 | tf_op jit(solution)/shard_map/ppermute | solution.py:54
  1878.7 47.5 %collective-permute-start.66 = (bf16[256,1152]{1,0:T(8,128)(2,1)S(1)}, bf16[256,1152]{1,0:T(8,128)(2,1)S(1)}, u32[]{:S(2)}, u32[]{:S(2)}) collective-permute-start(bf16[256,1152]{1,0:T(8,128)(2,1)S(1)} %multiply_convert_fusion.20), channel_id=1, source_target_pairs={{0,2},{1,3},{2,0},{3,1},{4,6},{5,7},{6,4},{7,5}} | collective-permute-start | bytes 1769480 | tf_op jit(solution)/shard_map/ppermute | solution.py:51
  1900.9 68.3 %collective-permute-start.62 = (bf16[256,1152]{1,0:T(8,128)(2,1)S(1)}, bf16[256,1152]{1,0:T(8,128)(2,1)S(1)}, u32[]{:S(2)}, u32[]{:S(2)}) collective-permute-start(bf16[256,1152]{1,0:T(8,128)(2,1)S(1)} %multiply_convert_fusion.21), channel_id=1, source_target_pairs={{0,1},{1,0},{2,3},{3,2},{4,5},{5,4},{6,7},{7,6}} | collective-permute-start | bytes 1769480 | tf_op jit(solution)/shard_map/ppermute | solution.py:54
  1938.9 44.2 %collective-permute-start.140 = (bf16[256,1152]{1,0:T(8,128)(2,1)S(1)}, bf16[256,1152]{1,0:T(8,128)(2,1)S(1)}, u32[]{:S(2)}, u32[]{:S(2)}) collective-permute-start(bf16[256,1152]{1,0:T(8,128)(2,1)S(1)} %multiply_convert_fusion.13), channel_id=1, source_target_pairs={{0,1},{1,0},{2,3},{3,2},{4,5},{5,4},{6,7},{7,6}} | collective-permute-start | bytes 1769480 | tf_op jit(solution)/shard_map/ppermute | solution.py:54
  1998.5 51.2 %collective-permute-start.142 = (f32[256,1280]{1,0:T(8,128)S(1)}, f32[256,1280]{1,0:T(8,128)S(1)}, u32[]{:S(2)}, u32[]{:S(2)}) collective-permute-start(f32[256,1280]{1,0:T(8,128)S(1)} %fusion.145), channel_id=1, source_target_pairs={{0,4},{4,0},{1,5},{5,1},{2,6},{6,2},{3,7},{7,3}} | collective-permute-start | bytes 3932168 | tf_op jit(solution)/shard_map/ppermute | solution.py:60
  (223 other events, 5094.6 us)

commit v2 on v0

v2 whole, which is shorter than its diff:
```python
import functools

import jax
import jax.numpy as jnp
from jax import lax
from jax.experimental import pallas as pl
from jax.experimental.pallas import tpu as pltpu
from jax.sharding import PartitionSpec as P

NORM_EPS = 1e-5
ROPE_BASE = 10000.0
NEG_BIG = -1e30
F32 = jnp.float32
BF16 = jnp.bfloat16
MESH = pl.DeviceIdType.MESH


def seg_positions(seg_rows):
    positions = jnp.arange(seg_rows.shape[-1], dtype=jnp.int32)
    previous = jnp.concatenate([seg_rows[..., :1] - 1, seg_rows[..., :-1]], axis=-1)
    start_at = jnp.where(seg_rows != previous, positions, 0)
    return positions - lax.cummax(start_at, axis=seg_rows.ndim - 1)


def rope_tables(positions, head_dim):
    half_dim = head_dim // 2
    inv_freq = ROPE_BASE ** (-2.0 * jnp.arange(half_dim, dtype=F32) / head_dim)
    angles = positions.astype(F32)[..., None] * inv_freq
    return jnp.cos(angles), jnp.sin(angles)


def mm(a, b):
    return jnp.dot(a, b, preferred_element_type=F32)


FEAT = 1280
EMBED = 5120
HALF = 1280
FHALF = 3456
ROWS = 256
QB = 256
GB = 384
SW = 768
N_Q = HALF // QB
N_G = FHALF // GB
D_CHUNK = 3 * GB
N_D = FHALF // D_CHUNK
CB = 256


def body(n_layers, x_ref, cos_ref, sin_ref, mask_ref, gain_ref, wq, wk, wv, wo, wg, wu, wd,
         out_ref, qkvr, gur,
         R, H, HC, XS, XO, XR, W, WR, ACT, PB, YR, SQ, SQC, SQS, SQX,
         xs_s, xr_s, as_s, ar_s, acs_s, acr_s, ys_s, yr_s, hys_s, hyr_s, hcs_s, hcr_s,
         sqcs_s, sqcr_s, sqxs_s, sqxr_s, sws_s, swr_s, os_s, or_s, w_s, wr_s):
    m = lax.axis_index('mp')
    t = lax.axis_index('tok')
    core = lax.rem(t, 2)
    xpos = lax.div(t, 2)
    t_c = xpos * 2 + (1 - core)
    t_x = (1 - xpos) * 2 + core
    t_d = (1 - xpos) * 2 + (1 - core)
    rep = lax.axis_index('rep')
    dev = {'c': (rep, m, t_c), 'x': (rep, m, t_x), 'd': (rep, m, t_d), 'y': (rep, 1 - m, t)}

    barrier = pltpu.get_barrier_semaphore()
    for k in ('c', 'x', 'd', 'y'):
        pl.semaphore_signal(barrier, inc=1, device_id=dev[k], device_id_type=MESH)
    pl.semaphore_wait(barrier, 4)

    def rcopy(src, dst, ss, rs, to):
        return pltpu.make_async_remote_copy(src_ref=src, dst_ref=dst, send_sem=ss, recv_sem=rs,
                                            device_id=dev[to], device_id_type=MESH)

    def al(v, n=128):
        return pl.multiple_of(v, n)

    swaps = {}
    n_sw = [0]

    def swap_start(key, src, dst):
        i = n_sw[0]
        n_sw[0] += 1
        c = rcopy(src, dst, sws_s.at[i], swr_s.at[i], 'c')
        c.start()
        swaps[key] = [c, False]

    def swap_need(key):
        e = swaps[key]
        if not e[1]:
            e[0].wait()
            e[1] = True

    def swap_qkv(l, fine):
        for b in range(N_Q):
            for i, w in enumerate((wq, wk, wv)):
                if fine:
                    swap_start((l, 'qkv', i, b), w.at[l, :, pl.ds(al((1 - core) * HALF + b * QB), QB)],
                               qkvr.at[l, i, :, pl.ds(b * QB, QB)])
                elif b == 0:
                    swap_start((l, 'qkv', i), w.at[l, :, pl.ds(al((1 - core) * HALF), HALF)], qkvr.at[l, i])
        if not fine:
            for b in range(N_Q):
                for i in range(3):
                    swaps[(l, 'qkv', i, b)] = swaps[(l, 'qkv', i)]

    def swap_gu(l):
        for i, w in enumerate((wg, wu)):
            swap_start((l, 'gu', i), w.at[l, :, pl.ds(al((1 - core) * FHALF), FHALF)], gur.at[l, i])

    steps = []
    for l in range(n_layers):
        for mb in range(2):
            steps += [(l, mb, 'q', b) for b in range(N_Q)]
        for mb in range(2):
            steps += [(l, mb, 'g', b) for b in range(N_G)]

    def w_copies(k):
        l, mb, kind, b = steps[k]
        s = k % 2
        cs = []
        if kind == 'q':
            for i, w in enumerate((wq, wk, wv)):
                cs.append((w.at[l, :, pl.ds(al(core * HALF + b * QB), QB)], W.at[s, 0, :, pl.ds(i * QB, QB)]))
                cs.append((qkvr.at[l, i, :, pl.ds(b * QB, QB)], W.at[s, 1, :, pl.ds(i * QB, QB)]))
        else:
            for i, w in enumerate((wg, wu)):
                cs.append((w.at[l, :, pl.ds(al(core * FHALF + b * GB), GB)], W.at[s, 0, :, pl.ds(i * GB, GB)]))
                cs.append((gur.at[l, i, :, pl.ds(b * GB, GB)], W.at[s, 1, :, pl.ds(i * GB, GB)]))
        return [pltpu.make_async_copy(a, d, w_s.at[s, j]) for j, (a, d) in enumerate(cs)]

    w_live = {}

    def w_start(k):
        if k >= len(steps):
            return
        l, mb, kind, b = steps[k]
        if kind == 'q':
            for i in range(3):
                swap_need((l, 'qkv', i, b))
        else:
            for i in range(2):
                swap_need((l, 'gu', i))
        w_live[k] = w_copies(k)
        for c in w_live[k]:
            c.start()

    x_live = {}

    def issue(k):
        l, mb, kind, b = steps[k]
        s = k % 2
        for c in w_live.pop(k):
            c.wait()
        if k >= 2:
            x_live[k - 2].wait_send()

        def half(row0, dst):
            @pl.loop(0, SW // CB)
            def _(j):
                cols = pl.ds(al(j * CB, CB), CB)
                dst[s, :, cols] = (mm(H[mb, pl.ds(row0, ROWS), :], W[s, 0, :, cols])
                                   + mm(HC[mb, pl.ds(row0, ROWS), :], W[s, 1, :, cols]))
        half(ROWS, XS)
        x_live[k] = rcopy(XS.at[s], XR.at[k % 4], xs_s.at[s], xr_s.at[k % 4], 'x')
        x_live[k].start()
        half(0, XO)
        w_start(k + 2)

    a_live = {}

    def consume(k):
        l, mb, kind, b = steps[k]
        s, q = k % 2, k % 4
        x_live[k].wait_recv()
        if kind == 'q':
            cos, sin = cos_ref[mb], sin_ref[mb]
            for hh in range(QB // 128):
                def part(i):
                    c0 = i * QB + hh * 128
                    return XO[s, :, c0:c0 + 128] + XR[q, :, c0:c0 + 128]

                def rope(v):
                    return (v * cos + pltpu.roll(v, 64, 1) * sin).astype(BF16)
                qh, kh, vh = rope(part(0)), rope(part(1)), part(2).astype(BF16)
                sc = lax.dot_general(qh, kh, (((1,), (1,)), ((), ())), preferred_element_type=F32) * (128 ** -0.5)
                sc = jnp.where(mask_ref[mb] > 0.0, sc, NEG_BIG)
                e = jnp.exp(sc - jnp.max(sc, axis=-1, keepdims=True))
                p = (e / jnp.sum(e, axis=-1, keepdims=True)).astype(BF16)
                ACT[mb, 0, :, b * QB + hh * 128:b * QB + hh * 128 + 128] = mm(p, vh).astype(BF16)
            cols = pl.ds(b * QB, QB)
        else:
            g = XO[s, :, :GB] + XR[q, :, :GB]
            u = XO[s, :, GB:] + XR[q, :, GB:]
            ACT[mb, 0, :, b * GB:(b + 1) * GB] = (jax.nn.silu(g) * u).astype(BF16)
            cols = pl.ds(b * GB, GB)
        c = rcopy(ACT.at[mb, 0, :, cols], ACT.at[mb, 1, :, cols], as_s.at[mb, b], ar_s.at[mb, b], 'x')
        c.start()
        a_live[mb, b] = c

    row_seq = []
    for l in range(n_layers):
        row_seq += [(l, mb, 'o', 0) for mb in range(2)] + [(l, mb, 'd', j) for mb in range(2) for j in range(N_D)]
    row_live = {}

    def row_start(i):
        if i >= len(row_seq):
            return
        l, mb, kind, j = row_seq[i]
        if kind == 'o':
            n, src = HALF, lambda c: wo.at[l, pl.ds(al(c * HALF), HALF), :]
        else:
            n, src = D_CHUNK, lambda c: wd.at[l, pl.ds(al(c * FHALF + j * D_CHUNK), D_CHUNK), :]
        row_live[i] = [pltpu.make_async_copy(src(core), WR.at[0, pl.ds(0, n), :], wr_s.at[0]),
                       pltpu.make_async_copy(src(1 - core), WR.at[1, pl.ds(0, n), :], wr_s.at[1])]
        for c in row_live[i]:
            c.start()

    row_at = [0]

    def row_wait():
        for c in row_live.pop(row_at[0]):
            c.wait()

    def row_done():
        row_at[0] += 1
        row_start(row_at[0])

    def row_mm(mb, xs, a0, n, first):
        @pl.loop(0, FEAT // CB)
        def _(j):
            cols = pl.ds(al(j * CB, CB), CB)
            v = (mm(ACT[mb, xs, :, a0:a0 + n], WR[0, :n, cols])
                 + mm(ACT[mb, 2 + xs, :, a0:a0 + n], WR[1, :n, cols]))
            if first:
                PB[mb, xs, :, cols] = v
            else:
                PB[mb, xs, :, cols] += v

    ac_live = {}

    def act_to_core(mb, xs, j, a0, n):
        cols = pl.ds(a0, n)
        c = rcopy(ACT.at[mb, xs, :, cols], ACT.at[mb, 2 + xs, :, cols], acs_s.at[mb, j, xs], acr_s.at[mb, j, xs], 'c')
        c.start()
        ac_live[mb, j, xs] = c

    y_live = {}

    def y_send(mb, xs):
        c = rcopy(PB.at[mb, xs, pl.ds(128, 128), :], YR.at[mb, xs], ys_s.at[mb, xs], yr_s.at[mb, xs], 'y')
        c.start()
        y_live[mb, xs] = c

    def r_update(mb):
        for xs in range(2):
            y_live[mb, xs].wait()
            rows = slice(xs * 128, xs * 128 + 128)
            R[mb, rows, :] = R[mb, rows, :] + (PB[mb, xs, :128, :] + YR[mb, xs])

    n_live = {}

    def norm_squares(mb):
        acc = None
        for j in range(FEAT // 128):
            v = R[mb, :, j * 128:(j + 1) * 128]
            acc = v * v if acc is None else acc + v * v
        SQ[mb] = acc
        c = rcopy(SQ.at[mb], SQC.at[mb], sqcs_s.at[mb], sqcr_s.at[mb], 'c')
        c.start()
        c.wait()
        SQS[mb] = SQ[mb] + SQC[mb]
        c = rcopy(SQS.at[mb], SQX.at[mb], sqxs_s.at[mb], sqxr_s.at[mb], 'x')
        c.start()
        n_live[mb, 'sq'] = c

    def norm_apply(mb, gi):
        n_live[mb, 'sq'].wait()
        for xs in range(2):
            o = 1 - xs
            tot = SQS[mb, xs * 128:(xs + 1) * 128, :] + SQX[mb, o * 128:(o + 1) * 128, :]
            scale = lax.rsqrt(jnp.sum(tot, axis=-1, keepdims=True) / EMBED + NORM_EPS)
            h = R[mb, xs * 128:(xs + 1) * 128, :] * scale * gain_ref[gi:gi + 1, :]
            H[mb, xs * 256:xs * 256 + 128, :] = h.astype(BF16)
        for xs in range(2):
            mine, theirs = pl.ds(xs * 256, 128), pl.ds(xs * 256 + 128, 128)
            c = rcopy(H.at[mb, mine, :], H.at[mb, theirs, :], hys_s.at[mb, xs], hyr_s.at[mb, xs], 'y')
            c.start()
            n_live[mb, 'y', xs] = c
        for xs in range(2):
            mine = pl.ds(xs * 256, 128)
            c = rcopy(H.at[mb, mine, :], HC.at[mb, mine, :], hcs_s.at[mb, xs], hcr_s.at[mb, xs], 'c')
            c.start()
            n_live[mb, 'c', xs] = c

    def norm_finish(mb):
        for xs in range(2):
            n_live[mb, 'y', xs].wait()
            theirs = pl.ds(xs * 256 + 128, 128)
            c = rcopy(H.at[mb, theirs, :], HC.at[mb, theirs, :], hcs_s.at[mb, 2 + xs], hcr_s.at[mb, 2 + xs], 'c')
            c.start()
            n_live[mb, 'c', 2 + xs] = c
        for i in range(4):
            n_live[mb, 'c', i].wait()

    o_live = []

    def out_send(mb):
        cols = pl.ds(al(t * FEAT), FEAT)
        for i, (xs, flip, to) in enumerate(((1, 0, 'x'), (1, 1, 'd'), (0, 1, 'c'))):
            cp = core + flip * (1 - 2 * core)
            c = rcopy(R.at[mb, pl.ds(al(xs * 128 + cp * 64, 64), 64), :], out_ref.at[mb, :, cols],
                      os_s.at[mb, i], or_s.at[mb, i], to)
            c.start()
            o_live.append(c)
        c = pltpu.make_async_copy(R.at[mb, pl.ds(al(core * 64, 64), 64), :], out_ref.at[mb, :, cols], os_s.at[mb, 3])
        c.start()
        o_live.append(c)

    todo = {}

    def at(k, f, *args):
        todo.setdefault(k, []).append(functools.partial(f, *args))

    def tail_a(l, mb, kind):
        if kind == 'q':
            j, a0, n, first = 0, 0, HALF, True
        else:
            j, a0, n, first = N_D - 1, (N_D - 1) * D_CHUNK, D_CHUNK, False
        act_to_core(mb, 0, j, a0, n)
        row_wait()
        ac_live[mb, j, 0].wait()
        row_mm(mb, 0, a0, n, first)
        y_send(mb, 0)

    def tail_b(l, mb, kind):
        if kind == 'q':
            j, a0, n, first, bs = 0, 0, HALF, True, range(N_Q)
        else:
            j, a0, n, first, bs = N_D - 1, (N_D - 1) * D_CHUNK, D_CHUNK, False, range(N_G - 3, N_G)
        for b in bs:
            a_live[mb, b].wait()
        act_to_core(mb, 1, j, a0, n)
        ac_live[mb, j, 1].wait()
        row_mm(mb, 1, a0, n, first)
        row_done()
        y_send(mb, 1)

    def down_mid(mb, j):
        a0 = j * D_CHUNK
        act_to_core(mb, 0, j, a0, D_CHUNK)
        for b in range(3 * j, 3 * j + 3):
            a_live[mb, b].wait()
        act_to_core(mb, 1, j, a0, D_CHUNK)
        row_wait()
        for xs in range(2):
            ac_live[mb, j, xs].wait()
            row_mm(mb, xs, a0, D_CHUNK, j == 0)
        row_done()

    def update_and_squares(mb):
        r_update(mb)
        norm_squares(mb)

    def finish_out(mb):
        r_update(mb)
        out_send(mb)

    n_steps = len(steps)
    for k, (l, mb, kind, b) in enumerate(steps):
        last = b == (N_Q if kind == 'q' else N_G) - 1
        if kind == 'g' and b % 3 == 2 and not last:
            at(k + 2, down_mid, mb, b // 3)
        if last:
            at(k + 1, tail_a, l, mb, kind)
            at(k + 2, tail_b, l, mb, kind)
            if kind == 'g' and l == n_layers - 1:
                at(k + 3, finish_out, mb)
            else:
                at(k + 3, update_and_squares, mb)
                at(k + 4, norm_apply, mb, 2 * l + 1 if kind == 'q' else 2 * l + 2)
                at(k + 5, norm_finish, mb)
    at(1, norm_squares, 1)
    at(2, norm_apply, 1, 0)
    at(3, norm_finish, 1)
    at(3, swap_gu, 0)
    if n_layers > 1:
        at(2 * N_Q + 7, swap_qkv, 1, False)
        at(2 * N_Q + 12, swap_gu, 1)

    for mb in range(2):
        R[mb] = x_ref[mb].astype(F32)
    norm_squares(0)
    swap_qkv(0, True)
    row_start(0)
    w_start(0)
    norm_apply(0, 0)
    norm_finish(0)
    w_start(1)
    for k in range(n_steps + 4):
        if k < n_steps:
            issue(k)
        if 1 <= k <= n_steps:
            consume(k - 1)
        for f in todo.pop(k, []):
            f()
    assert not todo
    for k in (n_steps - 2, n_steps - 1):
        x_live[k].wait_send()
    for c in o_live:
        c.wait()


def solution(mesh):
    act_spec = P(None, ('rep', 'tok', 'mp'), None)
    seg_spec = P(None, ('rep', 'tok', 'mp'))
    gain_spec = P(None, None)
    head_in = P(None, 'tok', 'mp', None)
    head_out = P(None, 'mp', None, 'tok')
    ffn_in = P(None, 'tok', 'mp')
    ffn_out = P(None, 'mp', 'tok')

    def to_t(v, bits):
        return lax.ppermute(v, 'tok', [(i, i ^ bits) for i in range(4)])

    def device_fn(x_in, seg_ids, g_attn, w_q, w_k, w_v, w_o, g_mlp, w_gate, w_up, w_down):
        n_layers = w_q.shape[0]
        micro_n, loc_len, embed = x_in.shape
        feat, heads, head_dim = w_q.shape[1:]
        t = lax.axis_index('tok')
        m = lax.axis_index('mp')
        core = t % 2
        xpos = t // 2

        seg_all = lax.all_gather(seg_ids, ('tok', 'mp'), axis=1, tiled=True)
        blk_len = 2 * loc_len
        seg_own = lax.dynamic_slice_in_dim(seg_all, xpos * 2 * blk_len, 2 * blk_len, 1).reshape(micro_n, 2, blk_len)
        pos_own = seg_positions(seg_own)
        in_blk = jnp.broadcast_to(jnp.arange(blk_len, dtype=jnp.int32), seg_own.shape)
        blk_id = jnp.broadcast_to(jnp.arange(2, dtype=jnp.int32)[:, None], seg_own.shape)

        def to_rows(v):
            v4 = v.reshape(micro_n, 2, 2, loc_len)
            v4 = jnp.where(m == 0, v4, v4[:, :, ::-1])
            return v4.transpose(0, 2, 1, 3).reshape(micro_n, 2 * blk_len)
        seg_r, pos_r, in_r, blk_r = to_rows(seg_own), to_rows(pos_own), to_rows(in_blk), to_rows(blk_id)

        def eq(v):
            return v[:, :, None] == v[:, None, :]
        allowed = eq(seg_r) & eq(blk_r) & (in_r[:, None, :] <= in_r[:, :, None])
        cos_t, sin_t = rope_tables(pos_r, head_dim)
        cos_f = jnp.concatenate([cos_t, cos_t], axis=-1)
        sin_f = jnp.concatenate([-sin_t, sin_t], axis=-1)

        def piece(k):
            s = lax.dynamic_slice_in_dim(x_in, (t ^ k) * feat, feat, 2)
            return to_t(s, k) if k else s
        p = [piece(k) for k in range(4)]
        lo = jnp.where(core == 0, jnp.stack([p[0], p[1], p[2], p[3]], 1), jnp.stack([p[1], p[0], p[3], p[2]], 1))
        x_rows = lo.reshape(micro_n, 4 * loc_len, feat)

        gains = jnp.stack([g[l] for l in range(n_layers) for g in (g_attn, g_mlp)])
        gains = lax.dynamic_slice_in_dim(gains, t * feat, feat, 1).astype(F32)
        flat_q, flat_k, flat_v = [w.reshape(n_layers, feat, heads * head_dim) for w in (w_q, w_k, w_v)]
        flat_o = w_o.reshape(n_layers, heads * head_dim, feat)

        vm = pl.BlockSpec(memory_space=pltpu.VMEM)
        hb = pl.BlockSpec(memory_space=pltpu.HBM)
        dma = pltpu.SemaphoreType.DMA
        out = pl.pallas_call(
            functools.partial(body, n_layers),
            out_shape=(jax.ShapeDtypeStruct((micro_n, loc_len, embed), F32),
                       jax.ShapeDtypeStruct((n_layers, 3, FEAT, HALF), BF16),
                       jax.ShapeDtypeStruct((n_layers, 2, FEAT, FHALF), BF16)),
            in_specs=[vm] * 5 + [hb] * 7,
            out_specs=(hb, hb, hb),
            scratch_shapes=[
                pltpu.VMEM((2, 256, FEAT), F32),
                pltpu.VMEM((2, 512, FEAT), BF16),
                pltpu.VMEM((2, 512, FEAT), BF16),
                pltpu.VMEM((2, ROWS, SW), F32),
                pltpu.VMEM((2, ROWS, SW), F32),
                pltpu.VMEM((4, ROWS, SW), F32),
                pltpu.VMEM((2, 2, FEAT, SW), BF16),
                pltpu.VMEM((2, HALF, FEAT), BF16),
                pltpu.VMEM((2, 4, ROWS, FHALF), BF16),
                pltpu.VMEM((2, 2, ROWS, FEAT), F32),
                pltpu.VMEM((2, 2, 128, FEAT), F32),
                pltpu.VMEM((2, 256, 128), F32),
                pltpu.VMEM((2, 256, 128), F32),
                pltpu.VMEM((2, 256, 128), F32),
                pltpu.VMEM((2, 256, 128), F32),
                dma((2,)), dma((4,)),
                dma((2, N_G)), dma((2, N_G)),
                dma((2, N_D, 2)), dma((2, N_D, 2)),
                dma((2, 2)), dma((2, 2)),
                dma((2, 2)), dma((2, 2)),
                dma((2, 4)), dma((2, 4)),
                dma((2,)), dma((2,)), dma((2,)), dma((2,)),
                dma((22,)), dma((22,)),
                dma((2, 4)), dma((2, 4)),
                dma((2, 6)), dma((2,)),
            ],
            compiler_params=pltpu.CompilerParams(collective_id=0, has_side_effects=True, vmem_limit_bytes=67043328),
        )(x_rows, cos_f, sin_f, allowed.astype(F32), gains, flat_q, flat_k, flat_v, flat_o, w_gate, w_up, w_down)
        return out[0]

    return jax.shard_map(
        device_fn,
        mesh=mesh,
        in_specs=(act_spec, seg_spec, gain_spec, head_in, head_in, head_in, head_out, gain_spec, ffn_in, ffn_in, ffn_out),
        out_specs=act_spec,
        check_vma=False,
    )
```

time: 4290 us -> 1410 us (0.33)
  waiting for transfers between devices: 3760 us -> 0.01 us
  Pallas kernels: 0 us -> 1260 us
  matrix products: 311 us -> 0 us
  local copies, waits for them, and re-layouts: 160 us -> 113 us
    all_gather x18 -> x0, waiting for transfers between devices: 3520 us -> none  [the longest x2 780 us: device_fn(): wg_full = lax.all_gather(w_gate[layer_idx], 'tok', axis=0, tiled=True)]
    pallas_call x0 -> x1, Pallas kernels: none -> 1260 us  [device_fn(): pl.pallas_call(functools.partial(body, n_layers), out_shape=(jax.ShapeDty...]
    dot_general x14 -> x0, matrix products: 303 us -> none  [the longest x2 71 us: device_fn(): jnp.einsum('mse,ef->msf', h_blk, wg_full, preferred_element_type=jnp.floa...]
    reduce_scatter x4 -> x0, waiting for transfers between devices: 241 us -> none  [device_fn(): lax.psum_scatter(part_sum, 'mp', scatter_dimension=1, tiled=True)]
    slice x7 -> x1, local copies, waits for them, and re-layouts: 118 us -> 0.06 us  [device_fn(): gains = jnp.stack([g[l] for l in range(n_layers) for g in (g_attn, g_mlp)])]
    reshape x0 -> x4, local copies, waits for them, and re-layouts: none -> 52.8 us  [the longest x3 52.8 us: device_fn(): w.reshape(n_layers, feat, heads * head_dim)]
  transfers between devices with their start and end apart: 22 -> 3, of which waited for: 20 -> 0; matrix products, arithmetic and copies ran while one was open for 9% -> 8% of each run, Pallas kernels for 0% -> 0%
where the time goes in v2:
time: 1410 us; the launch traced here: 1400 us
  Pallas kernels  1260 us (89%)
  local copies, waits for them, and re-layouts  113 us (8%)
  blocking collectives  21.6 us (2%)
    pallas_call x1, Pallas kernels, device_fn(): pl.pallas_call(functools.partial(body, n_layers), out_shape=(jax.ShapeDty...  1260 us
    unnamed x11, local copies, waits for them, and re-layouts  56.5 us
    reshape x3, local copies, waits for them, and re-layouts, device_fn(): w.reshape(n_layers, feat, heads * head_dim)  52.8 us
  transfers between devices with their start and end apart: 3, of which 0 were waited for; matrix products, arithmetic and copies ran while one was open for 8% of the time, Pallas kernels for 0%

profile of v2, /device:TPU:0, one launch (start us, length us, event | category | flops | bytes accessed | tf_op | source)
XLA Modules:
  0.0 1401.8 jit_solution(1682471723052152599)
XLA Ops:
  0.0 0.0 copy-start.2
  0.0 1.4 dynamic-slice_bitcast_fusion
  1.4 0.9 collective-permute-start
  2.3 2.6 collective-permute-start.2
  4.9 0.0 collective-permute-start.1
  4.9 0.0 copy-done.2
  4.9 21.6 %all-gather = s32[8,64,2]{1,2,0:T(2,128)S(1)} all-gather(s32[1,64,2]{1,2,0:T(2,128)S(1)} %bitcast.35), channel_id=1, replica_groups=mesh['rep'=1,'mp'=2,'tok'=4] {'tok','mp'}, dimensions={0}, use_global_device_ids=true | all-gather | bytes 4608 | tf_op jit(solution)/shard_map/all_gather | solution.py:435
  26.5 0.1 reshape.62
  26.6 0.1 reshape_reshape.3
  26.8 0.1 le.15
  26.9 0.1 eq.47
  27.0 0.1 compare_select_fusion
  27.1 0.6 reduce_window_max.12
  27.7 0.1 reduce_window_max.13
  27.8 0.1 eq.43
  27.9 0.1 convert_element_type.21
  28.0 1.0 fusion
  29.0 0.8 pad_maximum_fusion.cos_ref
  29.8 17.7 %copy.38 = bf16[2,1280,20,128]{1,3,2,0:T(8,128)(2,1)} copy(bf16[2,1280,20,128]{3,1,2,0:T(8,128)(2,1)} %param.14) | data formatting | bytes 26214400 | tf_op args[3]
  47.5 17.6 %copy.41.wq = bf16[2,1280,2560]{2,1,0:T(8,128)(2,1)} copy(bf16[2,1280,2560]{1,2,0:T(8,128)(2,1)} %bitcast.26) | data formatting | bytes 26214400 | tf_op jit(solution)/shard_map/reshape | solution.py:464
  65.1 17.7 %copy.39 = bf16[2,1280,20,128]{1,3,2,0:T(8,128)(2,1)} copy(bf16[2,1280,20,128]{3,1,2,0:T(8,128)(2,1)} %param.15) | data formatting | bytes 26214400 | tf_op args[4]
  82.7 17.6 %copy.42.wk = bf16[2,1280,2560]{2,1,0:T(8,128)(2,1)} copy(bf16[2,1280,2560]{1,2,0:T(8,128)(2,1)} %bitcast.27) | data formatting | bytes 26214400 | tf_op jit(solution)/shard_map/reshape | solution.py:464
  100.3 17.7 %copy.40 = bf16[2,1280,20,128]{1,3,2,0:T(8,128)(2,1)} copy(bf16[2,1280,20,128]{3,1,2,0:T(8,128)(2,1)} %param.16) | data formatting | bytes 26214400 | tf_op args[5]
  117.9 0.0 copy-start
  117.9 0.0 copy-start.1
  117.9 17.6 %copy.43.wv = bf16[2,1280,2560]{2,1,0:T(8,128)(2,1)} copy(bf16[2,1280,2560]{1,2,0:T(8,128)(2,1)} %bitcast.28) | data formatting | bytes 26214400 | tf_op jit(solution)/shard_map/reshape | solution.py:464
  135.6 0.0 copy-done
  135.6 0.0 copy-done.1
  135.6 0.1 fusion.6
  135.6 0.7 fusion.4.gain_ref
  136.4 0.8 pad_maximum_fusion.1.sin_ref
  137.2 1.1 and_convert_fusion.mask_ref
  138.3 0.0 collective-permute-done
  138.3 0.0 collective-permute-done.2
  138.3 0.0 collective-permute-done.1
  138.3 0.3 maximum_select_fusion
  138.6 1.2 copy.32
  139.8 1258.1 %shard_map.109 = (f32[2,64,5120]{2,1,0:T(8,128)}, bf16[2,3,1280,1280]{3,2,1,0:T(8,128)(2,1)}, bf16[2,2,1280,3456]{3,2,1,0:T(8,128)(2,1)}) custom-call(bf16[2,256,1280]{2,1,0:T(8,128)(2,1)} %bitcast.30, f32[2,256,128]{2,1,0:T(8,128)} %pad_maximum_fusion.cos_ref, f32[2,256,128]{2,1,0:T(8,128)} %pad_maximum_fusion.1.sin_ref, ...), custom_call_target="tpu_custom_call" | custom-call | tf_op jit(solution)/shard_map/pallas_call | solution.py:470
  1397.9 3.5 copy.45
  (19 shorter events, 0.2 us)
Async XLA Ops:
  0.0 4.9 copy-start.2
  1.4 136.9 %collective-permute-start = (bf16[2,64,1280]{2,1,0:T(8,128)(2,1)S(1)}, bf16[2,64,1280]{2,1,0:T(8,128)(2,1)S(1)}, u32[]{:S(2)}, u32[]{:S(2)}) collective-permute-start(bf16[2,64,1280]{2,1,0:T(8,128)(2,1)S(1)} %get-tuple-element.8), channel_id=1, source_target_pairs={{0,1},{1,0},{2,3},{3,2},{4,5},{5,4},{6,7},{7,6}} | collective-permute-start | bytes 983048 | tf_op jit(solution)/shard_map/ppermute | solution.py:424
  2.3 136.1 %collective-permute-start.2 = (bf16[2,64,1280]{2,1,0:T(8,128)(2,1)S(1)}, bf16[2,64,1280]{2,1,0:T(8,128)(2,1)S(1)}, u32[]{:S(2)}, u32[]{:S(2)}) collective-permute-start(bf16[2,64,1280]{2,1,0:T(8,128)(2,1)S(1)} %get-tuple-element.9), channel_id=1, source_target_pairs={{0,3},{1,2},{2,1},{3,0},{4,7},{5,6},{6,5},{7,4}} | collective-permute-start | bytes 983048 | tf_op jit(solution)/shard_map/ppermute | solution.py:424
  4.9 133.5 %collective-permute-start.1 = (bf16[2,64,1280]{2,1,0:T(8,128)(2,1)S(1)}, bf16[2,64,1280]{2,1,0:T(8,128)(2,1)S(1)}, u32[]{:S(2)}, u32[]{:S(2)}) collective-permute-start(bf16[2,64,1280]{2,1,0:T(8,128)(2,1)S(1)} %get-tuple-element.10), channel_id=1, source_target_pairs={{0,2},{1,3},{2,0},{3,1},{4,6},{5,7},{6,4},{7,5}} | collective-permute-start | bytes 983048 | tf_op jit(solution)/shard_map/ppermute | solution.py:424
  117.9 17.6 %copy-start = (bf16[2,5120]{1,0:T(2,128)(2,1)S(1)}, bf16[2,5120]{1,0:T(2,128)(2,1)}, u32[]{:S(2)}) copy-start(bf16[2,5120]{1,0:T(2,128)(2,1)} %param.13) | copy-start | bytes 61444
  117.9 17.6 %copy-start.1 = (bf16[2,5120]{1,0:T(2,128)(2,1)S(1)}, bf16[2,5120]{1,0:T(2,128)(2,1)}, u32[]{:S(2)}) copy-start(bf16[2,5120]{1,0:T(2,128)(2,1)} %param.18) | copy-start | bytes 61444

commit v3 on v2

--- a/solution.py
+++ b/solution.py
@@ -15,13 +15,6 @@
 MESH = pl.DeviceIdType.MESH
 
 
-def seg_positions(seg_rows):
-    positions = jnp.arange(seg_rows.shape[-1], dtype=jnp.int32)
-    previous = jnp.concatenate([seg_rows[..., :1] - 1, seg_rows[..., :-1]], axis=-1)
-    start_at = jnp.where(seg_rows != previous, positions, 0)
-    return positions - lax.cummax(start_at, axis=seg_rows.ndim - 1)
-
-
 def rope_tables(positions, head_dim):
     half_dim = head_dim // 2
     inv_freq = ROPE_BASE ** (-2.0 * jnp.arange(half_dim, dtype=F32) / head_dim)
@@ -36,6 +29,7 @@
 FEAT = 1280
 EMBED = 5120
 HALF = 1280
+HEADS = 10
 FHALF = 3456
 ROWS = 256
 QB = 256
@@ -50,9 +44,9 @@
 
 def body(n_layers, x_ref, cos_ref, sin_ref, mask_ref, gain_ref, wq, wk, wv, wo, wg, wu, wd,
          out_ref, qkvr, gur,
-         R, H, HC, XS, XO, XR, W, WR, ACT, PB, YR, SQ, SQC, SQS, SQX,
+         XB, R, H, HC, XS, XO, XR, W, WR, ACT, PB, YR, SQ, SQC, SQS, SQX,
          xs_s, xr_s, as_s, ar_s, acs_s, acr_s, ys_s, yr_s, hys_s, hyr_s, hcs_s, hcr_s,
-         sqcs_s, sqcr_s, sqxs_s, sqxr_s, sws_s, swr_s, os_s, or_s, w_s, wr_s):
+         sqcs_s, sqcr_s, sqxs_s, sqxr_s, sws_s, swr_s, os_s, or_s, xbs_s, xbr_s, w_s, wr_s):
     m = lax.axis_index('mp')
     t = lax.axis_index('tok')
     core = lax.rem(t, 2)
@@ -91,18 +85,16 @@
             e[0].wait()
             e[1] = True
 
-    def swap_qkv(l, fine):
-        for b in range(N_Q):
+    def swap_qkv(l, bs):
+        for b in bs:
             for i, w in enumerate((wq, wk, wv)):
-                if fine:
-                    swap_start((l, 'qkv', i, b), w.at[l, :, pl.ds(al((1 - core) * HALF + b * QB), QB)],
-                               qkvr.at[l, i, :, pl.ds(b * QB, QB)])
-                elif b == 0:
-                    swap_start((l, 'qkv', i), w.at[l, :, pl.ds(al((1 - core) * HALF), HALF)], qkvr.at[l, i])
-        if not fine:
+                swap_start((l, 'qkv', i, b), w.at[l, pl.ds((1 - core) * HEADS + b * 2, 2)], qkvr.at[l, i, pl.ds(b * 2, 2)])
+
+    def swap_qkv_whole(l):
+        for i, w in enumerate((wq, wk, wv)):
+            swap_start((l, 'qkv', i), w.at[l, pl.ds((1 - core) * HEADS, HEADS)], qkvr.at[l, i])
             for b in range(N_Q):
-                for i in range(3):
-                    swaps[(l, 'qkv', i, b)] = swaps[(l, 'qkv', i)]
+                swaps[(l, 'qkv', i, b)] = swaps[(l, 'qkv', i)]
 
     def swap_gu(l):
         for i, w in enumerate((wg, wu)):
@@ -121,8 +113,10 @@
         cs = []
         if kind == 'q':
             for i, w in enumerate((wq, wk, wv)):
-                cs.append((w.at[l, :, pl.ds(al(core * HALF + b * QB), QB)], W.at[s, 0, :, pl.ds(i * QB, QB)]))
-                cs.append((qkvr.at[l, i, :, pl.ds(b * QB, QB)], W.at[s, 1, :, pl.ds(i * QB, QB)]))
+                for hh in range(2):
+                    cols = pl.ds(i * QB + hh * 128, 128)
+                    cs.append((w.at[l, core * HEADS + b * 2 + hh], W.at[s, 0, :, cols]))
+                    cs.append((qkvr.at[l, i, b * 2 + hh], W.at[s, 1, :, cols]))
         else:
             for i, w in enumerate((wg, wu)):
                 cs.append((w.at[l, :, pl.ds(al(core * FHALF + b * GB), GB)], W.at[s, 0, :, pl.ds(i * GB, GB)]))
@@ -161,9 +155,13 @@
                 cols = pl.ds(al(j * CB, CB), CB)
                 dst[s, :, cols] = (mm(H[mb, pl.ds(row0, ROWS), :], W[s, 0, :, cols])
                                    + mm(HC[mb, pl.ds(row0, ROWS), :], W[s, 1, :, cols]))
+        norm_ready(mb, 1)
         half(ROWS, XS)
         x_live[k] = rcopy(XS.at[s], XR.at[k % 4], xs_s.at[s], xr_s.at[k % 4], 'x')
         x_live[k].start()
+        if k == 0:
+            w_start(1)
+        norm_ready(mb, 0)
         half(0, XO)
         w_start(k + 2)
 
@@ -247,16 +245,17 @@
 
     y_live = {}
 
-    def y_send(mb, xs):
-        c = rcopy(PB.at[mb, xs, pl.ds(128, 128), :], YR.at[mb, xs], ys_s.at[mb, xs], yr_s.at[mb, xs], 'y')
+    def y_send(mb, xs, hf):
+        cols = pl.ds(hf * (FEAT // 2), FEAT // 2)
+        c = rcopy(PB.at[mb, xs, pl.ds(128, 128), cols], YR.at[mb, xs, :, cols], ys_s.at[mb, xs, hf], yr_s.at[mb, xs, hf], 'y')
         c.start()
-        y_live[mb, xs] = c
-
-    def r_update(mb):
-        for xs in range(2):
-            y_live[mb, xs].wait()
-            rows = slice(xs * 128, xs * 128 + 128)
-            R[mb, rows, :] = R[mb, rows, :] + (PB[mb, xs, :128, :] + YR[mb, xs])
+        y_live[mb, xs, hf] = c
+
+    def r_update(mb, xs, hf):
+        y_live[mb, xs, hf].wait()
+        rows = slice(xs * 128, xs * 128 + 128)
+        cols = slice(hf * (FEAT // 2), (hf + 1) * (FEAT // 2))
+        R[mb, rows, cols] = R[mb, rows, cols] + (PB[mb, xs, :128, cols] + YR[mb, xs, :, cols])
 
     n_live = {}
 
@@ -282,40 +281,70 @@
             scale = lax.rsqrt(jnp.sum(tot, axis=-1, keepdims=True) / EMBED + NORM_EPS)
             h = R[mb, xs * 128:(xs + 1) * 128, :] * scale * gain_ref[gi:gi + 1, :]
             H[mb, xs * 256:xs * 256 + 128, :] = h.astype(BF16)
-        for xs in range(2):
+        for xs in (1, 0):
             mine, theirs = pl.ds(xs * 256, 128), pl.ds(xs * 256 + 128, 128)
             c = rcopy(H.at[mb, mine, :], H.at[mb, theirs, :], hys_s.at[mb, xs], hyr_s.at[mb, xs], 'y')
             c.start()
             n_live[mb, 'y', xs] = c
-        for xs in range(2):
+        for xs in (1, 0):
             mine = pl.ds(xs * 256, 128)
             c = rcopy(H.at[mb, mine, :], HC.at[mb, mine, :], hcs_s.at[mb, xs], hcr_s.at[mb, xs], 'c')
             c.start()
             n_live[mb, 'c', xs] = c
 
-    def norm_finish(mb):
-        for xs in range(2):
-            n_live[mb, 'y', xs].wait()
+    def norm_forward(mb, xs):
+        if (mb, 'y', xs) in n_live:
+            n_live.pop((mb, 'y', xs)).wait()
             theirs = pl.ds(xs * 256 + 128, 128)
             c = rcopy(H.at[mb, theirs, :], HC.at[mb, theirs, :], hcs_s.at[mb, 2 + xs], hcr_s.at[mb, 2 + xs], 'c')
             c.start()
             n_live[mb, 'c', 2 + xs] = c
+
+    def norm_ready(mb, xs):
+        norm_forward(mb, xs)
+        for i in (xs, 2 + xs):
+            if (mb, 'c', i) in n_live:
+                n_live.pop((mb, 'c', i)).wait()
+
+    def norm_finish(mb):
+        for xs in (1, 0):
+            norm_forward(mb, xs)
+        for xs in (1, 0):
+            norm_ready(mb, xs)
+
+    o_live = []
+
+    def out_send(mb, xs, hf):
+        fh = FEAT // 2
+        cols = pl.ds(al(t * FEAT + hf * fh), fh)
+        for flip in range(2):
+            cp = core + flip * (1 - 2 * core)
+            src = R.at[mb, pl.ds(al(xs * 128 + cp * 64, 64), 64), pl.ds(hf * fh, fh)]
+            to = ('self', 'c', 'x', 'd')[2 * xs + flip]
+            i = 2 * xs + flip
+            if to == 'self':
+                c = pltpu.make_async_copy(src, out_ref.at[mb, :, cols], os_s.at[mb, hf, i])
+            else:
+                c = rcopy(src, out_ref.at[mb, :, cols], os_s.at[mb, hf, i], or_s.at[mb, hf, i], to)
+            c.start()
+            o_live.append(c)
+
+    def x_send(mb):
+        for i, (k, xs) in enumerate((('x', 1), ('d', 1), ('c', 0), ('self', 0))):
+            to_t = {'x': t_x, 'd': t_d, 'c': t_c, 'self': t}[k]
+            src = x_ref.at[mb, :, pl.ds(al(to_t * FEAT), FEAT)]
+            dst = XB.at[mb, pl.ds(al(xs * 128 + core * 64, 64), 64), :]
+            if k == 'self':
+                c = pltpu.make_async_copy(src, dst, xbs_s.at[mb, i])
+            else:
+                c = rcopy(src, dst, xbs_s.at[mb, i], xbr_s.at[mb, i], k)
+            c.start()
+            n_live[mb, 'xb', i] = c
+
+    def x_take(mb):
         for i in range(4):
-            n_live[mb, 'c', i].wait()
-
-    o_live = []
-
-    def out_send(mb):
-        cols = pl.ds(al(t * FEAT), FEAT)
-        for i, (xs, flip, to) in enumerate(((1, 0, 'x'), (1, 1, 'd'), (0, 1, 'c'))):
-            cp = core + flip * (1 - 2 * core)
-            c = rcopy(R.at[mb, pl.ds(al(xs * 128 + cp * 64, 64), 64), :], out_ref.at[mb, :, cols],
-                      os_s.at[mb, i], or_s.at[mb, i], to)
-            c.start()
-            o_live.append(c)
-        c = pltpu.make_async_copy(R.at[mb, pl.ds(al(core * 64, 64), 64), :], out_ref.at[mb, :, cols], os_s.at[mb, 3])
-        c.start()
-        o_live.append(c)
+            n_live.pop((mb, 'xb', i)).wait()
+        R[mb] = XB[mb].astype(F32)
 
     todo = {}
 
@@ -331,7 +360,9 @@
         row_wait()
         ac_live[mb, j, 0].wait()
         row_mm(mb, 0, a0, n, first)
-        y_send(mb, 0)
+        y_send(mb, 0, 0)
+        if not (l == n_layers - 1 and kind == 'g'):
+            y_send(mb, 0, 1)
 
     def tail_b(l, mb, kind):
         if kind == 'q':
@@ -344,7 +375,10 @@
         ac_live[mb, j, 1].wait()
         row_mm(mb, 1, a0, n, first)
         row_done()
-        y_send(mb, 1)
+        y_send(mb, 1, 0)
+        y_send(mb, 1, 1)
+        if l == n_layers - 1 and kind == 'g':
+            y_send(mb, 0, 1)
 
     def down_mid(mb, j):
         a0 = j * D_CHUNK
@@ -359,12 +393,19 @@
         row_done()
 
     def update_and_squares(mb):
-        r_update(mb)
+        for xs in range(2):
+            for hf in range(2):
+                r_update(mb, xs, hf)
         norm_squares(mb)
 
     def finish_out(mb):
-        r_update(mb)
-        out_send(mb)
+        for xs, hf in ((1, 0), (1, 1), (0, 0), (0, 1)):
+            r_update(mb, xs, hf)
+            out_send(mb, xs, hf)
+
+    def first_squares(mb):
+        x_take(mb)
+        norm_squares(mb)
 
     n_steps = len(steps)
     for k, (l, mb, kind, b) in enumerate(steps):
@@ -380,23 +421,22 @@
                 at(k + 3, update_and_squares, mb)
                 at(k + 4, norm_apply, mb, 2 * l + 1 if kind == 'q' else 2 * l + 2)
                 at(k + 5, norm_finish, mb)
-    at(1, norm_squares, 1)
+    at(1, first_squares, 1)
     at(2, norm_apply, 1, 0)
     at(3, norm_finish, 1)
     at(3, swap_gu, 0)
     if n_layers > 1:
-        at(2 * N_Q + 7, swap_qkv, 1, False)
+        at(2 * N_Q + 7, swap_qkv_whole, 1)
         at(2 * N_Q + 12, swap_gu, 1)
 
-    for mb in range(2):
-        R[mb] = x_ref[mb].astype(F32)
-    norm_squares(0)
-    swap_qkv(0, True)
+    x_send(0)
+    swap_qkv(0, (0,))
     row_start(0)
+    first_squares(0)
+    x_send(1)
     w_start(0)
     norm_apply(0, 0)
-    norm_finish(0)
-    w_start(1)
+    swap_qkv(0, range(1, N_Q))
     for k in range(n_steps + 4):
         if k < n_steps:
             issue(k)
@@ -420,9 +460,6 @@
     ffn_in = P(None, 'tok', 'mp')
     ffn_out = P(None, 'mp', 'tok')
 
-    def to_t(v, bits):
-        return lax.ppermute(v, 'tok', [(i, i ^ bits) for i in range(4)])
-
     def device_fn(x_in, seg_ids, g_attn, w_q, w_k, w_v, w_o, g_mlp, w_gate, w_up, w_down):
         n_layers = w_q.shape[0]
         micro_n, loc_len, embed = x_in.shape
@@ -432,36 +469,24 @@
         core = t % 2
         xpos = t // 2
 
-        seg_all = lax.all_gather(seg_ids, ('tok', 'mp'), axis=1, tiled=True)
-        blk_len = 2 * loc_len
-        seg_own = lax.dynamic_slice_in_dim(seg_all, xpos * 2 * blk_len, 2 * blk_len, 1).reshape(micro_n, 2, blk_len)
-        pos_own = seg_positions(seg_own)
-        in_blk = jnp.broadcast_to(jnp.arange(blk_len, dtype=jnp.int32), seg_own.shape)
-        blk_id = jnp.broadcast_to(jnp.arange(2, dtype=jnp.int32)[:, None], seg_own.shape)
-
-        def to_rows(v):
-            v4 = v.reshape(micro_n, 2, 2, loc_len)
-            v4 = jnp.where(m == 0, v4, v4[:, :, ::-1])
-            return v4.transpose(0, 2, 1, 3).reshape(micro_n, 2 * blk_len)
-        seg_r, pos_r, in_r, blk_r = to_rows(seg_own), to_rows(pos_own), to_rows(in_blk), to_rows(blk_id)
-
-        def eq(v):
-            return v[:, :, None] == v[:, None, :]
-        allowed = eq(seg_r) & eq(blk_r) & (in_r[:, None, :] <= in_r[:, :, None])
+        seg_y = lax.ppermute(seg_ids, 'mp', [(0, 1), (1, 0)])
+        seg_c = lax.ppermute(seg_ids, 'tok', [(i, i ^ 1) for i in range(4)])
+        seg_yc = lax.ppermute(seg_ids, ('mp', 'tok'), [(i, i ^ 5) for i in range(8)])
+        mine, theirs = jnp.stack([seg_ids, seg_y], 1), jnp.stack([seg_c, seg_yc], 1)
+        seg_r = jnp.where(core == 0, jnp.stack([mine, theirs], 2), jnp.stack([theirs, mine], 2)).reshape(micro_n, 4 * loc_len)
+        row = jnp.arange(4 * loc_len, dtype=jnp.int32)
+        in_r = ((row // (2 * loc_len)) ^ m) * loc_len + row % loc_len
+        blk_r = (row // loc_len) % 2
+        allowed = ((seg_r[:, :, None] == seg_r[:, None, :]) & (blk_r[:, None] == blk_r[None, :])
+                   & (in_r[None, :] <= in_r[:, None]))
+        pos_r = jnp.sum(allowed.astype(jnp.int32), axis=-1) - 1
         cos_t, sin_t = rope_tables(pos_r, head_dim)
         cos_f = jnp.concatenate([cos_t, cos_t], axis=-1)
         sin_f = jnp.concatenate([-sin_t, sin_t], axis=-1)
 
-        def piece(k):
-            s = lax.dynamic_slice_in_dim(x_in, (t ^ k) * feat, feat, 2)
-            return to_t(s, k) if k else s
-        p = [piece(k) for k in range(4)]
-        lo = jnp.where(core == 0, jnp.stack([p[0], p[1], p[2], p[3]], 1), jnp.stack([p[1], p[0], p[3], p[2]], 1))
-        x_rows = lo.reshape(micro_n, 4 * loc_len, feat)
-
         gains = jnp.stack([g[l] for l in range(n_layers) for g in (g_attn, g_mlp)])
         gains = lax.dynamic_slice_in_dim(gains, t * feat, feat, 1).astype(F32)
-        flat_q, flat_k, flat_v = [w.reshape(n_layers, feat, heads * head_dim) for w in (w_q, w_k, w_v)]
+        by_head = [w.transpose(0, 2, 1, 3) for w in (w_q, w_k, w_v)]
         flat_o = w_o.reshape(n_layers, heads * head_dim, feat)
 
         vm = pl.BlockSpec(memory_space=pltpu.VMEM)
@@ -470,11 +495,12 @@
         out = pl.pallas_call(
             functools.partial(body, n_layers),
             out_shape=(jax.ShapeDtypeStruct((micro_n, loc_len, embed), F32),
-                       jax.ShapeDtypeStruct((n_layers, 3, FEAT, HALF), BF16),
+                       jax.ShapeDtypeStruct((n_layers, 3, HEADS, FEAT, 128), BF16),
                        jax.ShapeDtypeStruct((n_layers, 2, FEAT, FHALF), BF16)),
-            in_specs=[vm] * 5 + [hb] * 7,
+            in_specs=[hb] + [vm] * 4 + [hb] * 7,
             out_specs=(hb, hb, hb),
             scratch_shapes=[
+                pltpu.VMEM((2, 256, FEAT), BF16),
                 pltpu.VMEM((2, 256, FEAT), F32),
                 pltpu.VMEM((2, 512, FEAT), BF16),
                 pltpu.VMEM((2, 512, FEAT), BF16),
@@ -493,16 +519,17 @@
                 dma((2,)), dma((4,)),
                 dma((2, N_G)), dma((2, N_G)),
                 dma((2, N_D, 2)), dma((2, N_D, 2)),
-                dma((2, 2)), dma((2, 2)),
+                dma((2, 2, 2)), dma((2, 2, 2)),
                 dma((2, 2)), dma((2, 2)),
                 dma((2, 4)), dma((2, 4)),
                 dma((2,)), dma((2,)), dma((2,)), dma((2,)),
                 dma((22,)), dma((22,)),
+                dma((2, 2, 4)), dma((2, 2, 4)),
                 dma((2, 4)), dma((2, 4)),
-                dma((2, 6)), dma((2,)),
+                dma((2, 12)), dma((2,)),
             ],
             compiler_params=pltpu.CompilerParams(collective_id=0, has_side_effects=True, vmem_limit_bytes=67043328),
-        )(x_rows, cos_f, sin_f, allowed.astype(F32), gains, flat_q, flat_k, flat_v, flat_o, w_gate, w_up, w_down)
+        )(x_in, cos_f, sin_f, allowed.astype(F32), gains, *by_head, flat_o, w_gate, w_up, w_down)
         return out[0]
 
     return jax.shard_map(

time: 1410 us -> 1270 us (0.901)
  local copies, waits for them, and re-layouts: 113 us -> 4.45 us
  blocking collectives: 21.6 us -> 0 us
    unnamed x11 -> x1, local copies, waits for them, and re-layouts: 56.5 us -> 3.48 us
    reshape x4 -> x0, local copies, waits for them, and re-layouts: 52.8 us -> none  [the longest x3 52.8 us: device_fn(): w.reshape(n_layers, feat, heads * head_dim)]
    all_gather x1 -> x0, blocking collectives: 21.6 us -> none  [device_fn(): seg_all = lax.all_gather(seg_ids, ('tok', 'mp'), axis=1, tiled=True)]
  transfers between devices with their start and end apart: 3 -> 3, of which waited for: 0 -> 1; matrix products, arithmetic and copies ran while one was open for 8% -> 0% of each run, Pallas kernels for 0% -> 0%
where the time goes in v3:
time: 1270 us
  Pallas kernels  1250 us (98%)
    pallas_call x1, Pallas kernels, device_fn(): pl.pallas_call(functools.partial(body, n_layers), out_shape=(jax.ShapeDty...  1250 us
  transfers between devices with their start and end apart: 3, of which 1 were waited for; matrix products, arithmetic and copies ran while one was open for 0% of the time, Pallas kernels for 0%

profile of v3, /device:TPU:0, one launch (start us, length us, event | category | flops | bytes accessed | tf_op | source)
XLA Modules:
  0.0 1266.2 jit_solution(14902471197396029638)
XLA Ops:
  0.0 3.4 collective-permute-start
  3.4 0.0 collective-permute-start.2
  3.4 0.1 collective-permute-start.1
  3.5 0.1 broadcast_compare_fusion.1
  3.6 0.1 broadcast_compare_fusion
  3.7 0.9 fusion.13
  4.6 0.7 fusion.5.gain_ref
  5.3 0.0 collective-permute-done
  5.3 0.7 add_bitcast_fusion
  6.0 0.4 collective-permute-done.2
  6.4 0.0 collective-permute-done.1
  6.4 0.1 select_n.82
  6.5 0.3 convert_reduce_fusion
  6.8 1.0 fusion.mask_ref
  7.8 1.0 fusion.1
  8.8 0.9 pad_maximum_fusion.cos_ref
  9.6 0.9 pad_maximum_fusion.1.sin_ref
  10.5 1252.0 %shard_map.109 = (f32[2,64,5120]{2,1,0:T(8,128)}, bf16[2,3,10,1280,128]{4,3,2,1,0:T(8,128)(2,1)}, bf16[2,2,1280,3456]{3,2,1,0:T(8,128)(2,1)}) custom-call(bf16[2,64,5120]{2,1,0:T(8,128)(2,1)} %x_ref.1, f32[2,256,128]{2,1,0:T(8,128)} %pad_maximum_fusion.cos_ref, f32[2,256,128]{2,1,0:T(8,128)} %pad_maximum_fusion.1.sin_ref, f32[2,256,256]{2,1,0:T(8,128)} %fusion.mask_ref, ...), custom_call_target="tpu_custom_call" | custom-call | tf_op jit(solution)/shard_map/pallas_call | solution.py:495
  1262.5 3.5 copy.14
  (6 shorter events, 0.0 us)
Async XLA Ops:
  0.0 5.3 collective-permute-start
  3.4 3.0 collective-permute-start.2
  3.4 3.0 collective-permute-start.1

commit v4 on v3

--- a/solution.py
+++ b/solution.py
@@ -2,6 +2,7 @@
 
 import jax
 import jax.numpy as jnp
+import numpy as np
 from jax import lax
 from jax.experimental import pallas as pl
 from jax.experimental.pallas import tpu as pltpu
@@ -15,11 +16,12 @@
 MESH = pl.DeviceIdType.MESH
 
 
-def rope_tables(positions, head_dim):
+def rope_rows(n_pos, head_dim):
     half_dim = head_dim // 2
-    inv_freq = ROPE_BASE ** (-2.0 * jnp.arange(half_dim, dtype=F32) / head_dim)
-    angles = positions.astype(F32)[..., None] * inv_freq
-    return jnp.cos(angles), jnp.sin(angles)
+    inv_freq = np.float32(ROPE_BASE) ** (np.float32(-2.0) * np.arange(half_dim, dtype=np.float32) / np.float32(head_dim))
+    angles = np.arange(n_pos, dtype=np.float32)[:, None] * inv_freq.astype(np.float32)
+    cos_t, sin_t = np.cos(angles), np.sin(angles)
+    return np.concatenate([cos_t, cos_t], axis=-1), np.concatenate([-sin_t, sin_t], axis=-1)
 
 
 def mm(a, b):
@@ -42,11 +44,11 @@
 CB = 256
 
 
-def body(n_layers, x_ref, cos_ref, sin_ref, mask_ref, gain_ref, wq, wk, wv, wo, wg, wu, wd,
+def body(n_layers, x_ref, seg_ref, ctab_ref, stab_ref, ga_ref, gm_ref, wq, wk, wv, wo, wg, wu, wd,
          out_ref, qkvr, gur,
-         XB, R, H, HC, XS, XO, XR, W, WR, ACT, PB, YR, SQ, SQC, SQS, SQX,
+         SEG, cos_ref, sin_ref, mask_ref, XB, R, H, HC, XS, XO, XR, W, WR, ACT, PB, YR, SQ, SQC, SQS, SQX,
          xs_s, xr_s, as_s, ar_s, acs_s, acr_s, ys_s, yr_s, hys_s, hyr_s, hcs_s, hcr_s,
-         sqcs_s, sqcr_s, sqxs_s, sqxr_s, sws_s, swr_s, os_s, or_s, xbs_s, xbr_s, w_s, wr_s):
+         sqcs_s, sqcr_s, sqxs_s, sqxr_s, sws_s, swr_s, os_s, or_s, xbs_s, xbr_s, sgs_s, sgr_s, w_s, wr_s):
     m = lax.axis_index('mp')
     t = lax.axis_index('tok')
     core = lax.rem(t, 2)
@@ -55,12 +57,12 @@
     t_x = (1 - xpos) * 2 + core
     t_d = (1 - xpos) * 2 + (1 - core)
     rep = lax.axis_index('rep')
-    dev = {'c': (rep, m, t_c), 'x': (rep, m, t_x), 'd': (rep, m, t_d), 'y': (rep, 1 - m, t)}
+    dev = {'c': (rep, m, t_c), 'x': (rep, m, t_x), 'd': (rep, m, t_d), 'y': (rep, 1 - m, t), 'yc': (rep, 1 - m, t_c)}
 
     barrier = pltpu.get_barrier_semaphore()
-    for k in ('c', 'x', 'd', 'y'):
+    for k in ('c', 'x', 'd', 'y', 'yc'):
         pl.semaphore_signal(barrier, inc=1, device_id=dev[k], device_id_type=MESH)
-    pl.semaphore_wait(barrier, 4)
+    pl.semaphore_wait(barrier, 5)
 
     def rcopy(src, dst, ss, rs, to):
         return pltpu.make_async_remote_copy(src_ref=src, dst_ref=dst, send_sem=ss, recv_sem=rs,
@@ -264,7 +266,7 @@
         for j in range(FEAT // 128):
             v = R[mb, :, j * 128:(j + 1) * 128]
             acc = v * v if acc is None else acc + v * v
-        SQ[mb] = acc
+        SQ[mb] = jnp.broadcast_to(jnp.sum(acc.T, axis=0, keepdims=True), (8, ROWS))
         c = rcopy(SQ.at[mb], SQC.at[mb], sqcs_s.at[mb], sqcr_s.at[mb], 'c')
         c.start()
         c.wait()
@@ -275,11 +277,13 @@
 
     def norm_apply(mb, gi):
         n_live[mb, 'sq'].wait()
+        g_ref = gm_ref if gi % 2 else ga_ref
+        gain = g_ref[gi // 2:gi // 2 + 1, pl.ds(al(t * FEAT), FEAT)].astype(F32)
         for xs in range(2):
             o = 1 - xs
-            tot = SQS[mb, xs * 128:(xs + 1) * 128, :] + SQX[mb, o * 128:(o + 1) * 128, :]
-            scale = lax.rsqrt(jnp.sum(tot, axis=-1, keepdims=True) / EMBED + NORM_EPS)
-            h = R[mb, xs * 128:(xs + 1) * 128, :] * scale * gain_ref[gi:gi + 1, :]
+            tot = SQS[mb, 0:1, xs * 128:(xs + 1) * 128] + SQX[mb, 0:1, o * 128:(o + 1) * 128]
+            scale = jnp.broadcast_to(lax.rsqrt(tot / EMBED + NORM_EPS), (128, 128)).T[:, 0:1]
+            h = R[mb, xs * 128:(xs + 1) * 128, :] * scale * gain
             H[mb, xs * 256:xs * 256 + 128, :] = h.astype(BF16)
         for xs in (1, 0):
             mine, theirs = pl.ds(xs * 256, 128), pl.ds(xs * 256 + 128, 128)
@@ -346,10 +350,47 @@
             n_live.pop((mb, 'xb', i)).wait()
         R[mb] = XB[mb].astype(F32)
 
+    def seg_send(mb):
+        for i, (k, mm_half) in enumerate((('y', 1), ('yc', 1), ('c', 0), ('self', 0))):
+            dst = SEG.at[mb, pl.ds(al(mm_half * 128 + core * 64, 64), 64), :]
+            if k == 'self':
+                c = pltpu.make_async_copy(seg_ref.at[mb], dst, sgs_s.at[mb, i])
+            else:
+                c = rcopy(seg_ref.at[mb], dst, sgs_s.at[mb, i], sgr_s.at[mb, i], k)
+            c.start()
+            n_live[mb, 'seg', i] = c
+
+    def tables(mb):
+        for i in range(4):
+            n_live.pop((mb, 'seg', i)).wait()
+        seg = SEG[mb]
+        same = None
+        for v in ((seg >> 12).astype(F32), (seg & 4095).astype(F32)):
+            e = v[:, 0:1] == v.T[0:1, :]
+            same = e if same is None else same & e
+        r = lax.broadcasted_iota(jnp.int32, (ROWS, ROWS), 0)
+        c = lax.broadcasted_iota(jnp.int32, (ROWS, ROWS), 1)
+
+        def place(v):
+            return ((v >> 7) ^ m) * 64 + (v & 63)
+        same = same & (((r >> 6) & 1) == ((c >> 6) & 1)) & (place(c) <= place(r))
+        allowed = jnp.where(same, 1.0, 0.0)
+        mask_ref[mb] = allowed
+        pos = jnp.sum(allowed, axis=-1, keepdims=True) - 1.0
+        lane = lax.broadcasted_iota(jnp.int32, (ROWS, 128), 1).astype(F32)
+        pick = jnp.where(lane == pos, 1.0, 0.0)
+        for tab, dst in ((ctab_ref, cos_ref), (stab_ref, sin_ref)):
+            dst[mb] = jnp.dot(pick, tab[...], preferred_element_type=F32, precision=lax.Precision.HIGHEST)
+
     todo = {}
+
+    early = {}
 
     def at(k, f, *args):
         todo.setdefault(k, []).append(functools.partial(f, *args))
+
+    def before(k, f, *args):
+        early.setdefault(k, []).append(functools.partial(f, *args))
 
     def tail_a(l, mb, kind):
         if kind == 'q':
@@ -398,8 +439,18 @@
                 r_update(mb, xs, hf)
         norm_squares(mb)
 
+    pieces = ((1, 0), (1, 1), (0, 0), (0, 1))
+
+    def finish(mb):
+        for xs, hf in pieces:
+            r_update(mb, xs, hf)
+
+    def send_finished(mb):
+        for xs, hf in pieces:
+            out_send(mb, xs, hf)
+
     def finish_out(mb):
-        for xs, hf in ((1, 0), (1, 1), (0, 0), (0, 1)):
+        for xs, hf in pieces:
             r_update(mb, xs, hf)
             out_send(mb, xs, hf)
 
@@ -408,20 +459,23 @@
         norm_squares(mb)
 
     n_steps = len(steps)
+    at(n_steps, send_finished, 0)
     for k, (l, mb, kind, b) in enumerate(steps):
         last = b == (N_Q if kind == 'q' else N_G) - 1
         if kind == 'g' and b % 3 == 2 and not last:
-            at(k + 2, down_mid, mb, b // 3)
+            before(k + 3, down_mid, mb, b // 3)
         if last:
-            at(k + 1, tail_a, l, mb, kind)
-            at(k + 2, tail_b, l, mb, kind)
+            before(k + 2, tail_a, l, mb, kind)
+            before(k + 3, tail_b, l, mb, kind)
             if kind == 'g' and l == n_layers - 1:
-                at(k + 3, finish_out, mb)
+                at(k + 3, finish if mb == 0 else finish_out, mb)
             else:
                 at(k + 3, update_and_squares, mb)
                 at(k + 4, norm_apply, mb, 2 * l + 1 if kind == 'q' else 2 * l + 2)
                 at(k + 5, norm_finish, mb)
+    at(0, tables, 0)
     at(1, first_squares, 1)
+    at(4, tables, 1)
     at(2, norm_apply, 1, 0)
     at(3, norm_finish, 1)
     at(3, swap_gu, 0)
@@ -430,6 +484,8 @@
         at(2 * N_Q + 12, swap_gu, 1)
 
     x_send(0)
+    for mb in range(2):
+        seg_send(mb)
     swap_qkv(0, (0,))
     row_start(0)
     first_squares(0)
@@ -440,11 +496,13 @@
     for k in range(n_steps + 4):
         if k < n_steps:
             issue(k)
+        for f in early.pop(k, []):
+            f()
         if 1 <= k <= n_steps:
             consume(k - 1)
         for f in todo.pop(k, []):
             f()
-    assert not todo
+    assert not todo and not early
     for k in (n_steps - 2, n_steps - 1):
         x_live[k].wait_send()
     for c in o_live:
@@ -464,28 +522,8 @@
         n_layers = w_q.shape[0]
         micro_n, loc_len, embed = x_in.shape
         feat, heads, head_dim = w_q.shape[1:]
-        t = lax.axis_index('tok')
-        m = lax.axis_index('mp')
-        core = t % 2
-        xpos = t // 2
-
-        seg_y = lax.ppermute(seg_ids, 'mp', [(0, 1), (1, 0)])
-        seg_c = lax.ppermute(seg_ids, 'tok', [(i, i ^ 1) for i in range(4)])
-        seg_yc = lax.ppermute(seg_ids, ('mp', 'tok'), [(i, i ^ 5) for i in range(8)])
-        mine, theirs = jnp.stack([seg_ids, seg_y], 1), jnp.stack([seg_c, seg_yc], 1)
-        seg_r = jnp.where(core == 0, jnp.stack([mine, theirs], 2), jnp.stack([theirs, mine], 2)).reshape(micro_n, 4 * loc_len)
-        row = jnp.arange(4 * loc_len, dtype=jnp.int32)
-        in_r = ((row // (2 * loc_len)) ^ m) * loc_len + row % loc_len
-        blk_r = (row // loc_len) % 2
-        allowed = ((seg_r[:, :, None] == seg_r[:, None, :]) & (blk_r[:, None] == blk_r[None, :])
-                   & (in_r[None, :] <= in_r[:, None]))
-        pos_r = jnp.sum(allowed.astype(jnp.int32), axis=-1) - 1
-        cos_t, sin_t = rope_tables(pos_r, head_dim)
-        cos_f = jnp.concatenate([cos_t, cos_t], axis=-1)
-        sin_f = jnp.concatenate([-sin_t, sin_t], axis=-1)
-
-        gains = jnp.stack([g[l] for l in range(n_layers) for g in (g_attn, g_mlp)])
-        gains = lax.dynamic_slice_in_dim(gains, t * feat, feat, 1).astype(F32)
+        seg_b = jnp.broadcast_to(seg_ids[:, :, None], (micro_n, loc_len, 128))
+        cos_rows, sin_rows = rope_rows(2 * loc_len, head_dim)
         by_head = [w.transpose(0, 2, 1, 3) for w in (w_q, w_k, w_v)]
         flat_o = w_o.reshape(n_layers, heads * head_dim, feat)
 
@@ -497,9 +535,13 @@
             out_shape=(jax.ShapeDtypeStruct((micro_n, loc_len, embed), F32),
                        jax.ShapeDtypeStruct((n_layers, 3, HEADS, FEAT, 128), BF16),
                        jax.ShapeDtypeStruct((n_layers, 2, FEAT, FHALF), BF16)),
-            in_specs=[hb] + [vm] * 4 + [hb] * 7,
+            in_specs=[hb] * 2 + [vm] * 4 + [hb] * 7,
             out_specs=(hb, hb, hb),
             scratch_shapes=[
+                pltpu.VMEM((2, ROWS, 128), jnp.int32),
+                pltpu.VMEM((2, ROWS, 128), F32),
+                pltpu.VMEM((2, ROWS, 128), F32),
+                pltpu.VMEM((2, ROWS, ROWS), F32),
                 pltpu.VMEM((2, 256, FEAT), BF16),
                 pltpu.VMEM((2, 256, FEAT), F32),
                 pltpu.VMEM((2, 512, FEAT), BF16),
@@ -512,10 +554,10 @@
                 pltpu.VMEM((2, 4, ROWS, FHALF), BF16),
                 pltpu.VMEM((2, 2, ROWS, FEAT), F32),
                 pltpu.VMEM((2, 2, 128, FEAT), F32),
-                pltpu.VMEM((2, 256, 128), F32),
-                pltpu.VMEM((2, 256, 128), F32),
-                pltpu.VMEM((2, 256, 128), F32),
-                pltpu.VMEM((2, 256, 128), F32),
+                pltpu.VMEM((2, 8, ROWS), F32),
+                pltpu.VMEM((2, 8, ROWS), F32),
+                pltpu.VMEM((2, 8, ROWS), F32),
+                pltpu.VMEM((2, 8, ROWS), F32),
                 dma((2,)), dma((4,)),
                 dma((2, N_G)), dma((2, N_G)),
                 dma((2, N_D, 2)), dma((2, N_D, 2)),
@@ -526,10 +568,11 @@
                 dma((22,)), dma((22,)),
                 dma((2, 2, 4)), dma((2, 2, 4)),
                 dma((2, 4)), dma((2, 4)),
+                dma((2, 4)), dma((2, 4)),
                 dma((2, 12)), dma((2,)),
             ],
             compiler_params=pltpu.CompilerParams(collective_id=0, has_side_effects=True, vmem_limit_bytes=67043328),
-        )(x_in, cos_f, sin_f, allowed.astype(F32), gains, *by_head, flat_o, w_gate, w_up, w_down)
+        )(x_in, seg_b, cos_rows, sin_rows, g_attn, g_mlp, *by_head, flat_o, w_gate, w_up, w_down)
         return out[0]
 
     return jax.shard_map(

time: 1270 us -> 1230 us (0.969)
  Pallas kernels: 1250 us -> 1220 us
    pallas_call x1, Pallas kernels: 1250 us -> 1220 us  [device_fn(): pl.pallas_call(functools.partial(body, n_layers), out_shape=(jax.ShapeDty...]
  transfers between devices with their start and end apart: 3 -> 0, of which waited for: 1 -> 0; matrix products, arithmetic and copies ran while one was open for 0% -> 0% of each run, Pallas kernels for 0% -> 0%
where the time goes in v4:
time: 1230 us; the launch traced here: 1220 us
  Pallas kernels  1220 us (99%)
    pallas_call x1, Pallas kernels, device_fn(): pl.pallas_call(functools.partial(body, n_layers), out_shape=(jax.ShapeDty...  1220 us

profile of v4, /device:TPU:0, one launch (start us, length us, event | category | flops | bytes accessed | tf_op | source)
XLA Modules:
  0.0 1223.4 jit_solution(1028694829214992459)
XLA Ops:
  0.0 1.4 broadcast_in_dim.2.seg_ref
  1.4 1218.2 %shard_map.127 = (f32[2,64,5120]{2,1,0:T(8,128)}, bf16[2,3,10,1280,128]{4,3,2,1,0:T(8,128)(2,1)}, bf16[2,2,1280,3456]{3,2,1,0:T(8,128)(2,1)}) custom-call(bf16[2,64,5120]{2,1,0:T(8,128)(2,1)} %x_ref.1, s32[2,64,128]{2,1,0:T(8,128)} %broadcast_in_dim.2.seg_ref, f32[128,128]{1,0:T(8,128)} %constant.4.clone.ctab_ref, f32[128,128]{1,0:T(8,128)} %constant.5.clone.stab_ref, ...), custom_call_target="tpu_custom_call" | custom-call | tf_op jit(solution)/shard_map/pallas_call | solution.py:533
  1219.5 3.5 copy.15

commit v5 on v4

--- a/solution.py
+++ b/solution.py
@@ -46,7 +46,7 @@
 
 def body(n_layers, x_ref, seg_ref, ctab_ref, stab_ref, ga_ref, gm_ref, wq, wk, wv, wo, wg, wu, wd,
          out_ref, qkvr, gur,
-         SEG, cos_ref, sin_ref, mask_ref, XB, R, H, HC, XS, XO, XR, W, WR, ACT, PB, YR, SQ, SQC, SQS, SQX,
+         SEG, cos_ref, sin_ref, mask_ref, XB, R, H, HC, XP, XR, W, WR, ACT, PB, YR, SQ, SQC, SQS, SQX,
          xs_s, xr_s, as_s, ar_s, acs_s, acr_s, ys_s, yr_s, hys_s, hyr_s, hcs_s, hcr_s,
          sqcs_s, sqcr_s, sqxs_s, sqxr_s, sws_s, swr_s, os_s, or_s, xbs_s, xbr_s, sgs_s, sgr_s, w_s, wr_s):
     m = lax.axis_index('mp')
@@ -151,20 +151,34 @@
         if k >= 2:
             x_live[k - 2].wait_send()
 
-        def half(row0, dst):
-            @pl.loop(0, SW // CB)
+        def half(j, xs):
+            cols = pl.ds(al(j * CB, CB), CB)
+            rows = pl.ds(al(xs * ROWS, ROWS), ROWS)
+            XP[s, xs, :, cols] = mm(H[mb, rows, :], W[s, 0, :, cols]) + mm(HC[mb, rows, :], W[s, 1, :, cols])
+        n = SW // CB
+        norm_ready(mb, 1)
+        x_live[k] = rcopy(XP.at[s, 1], XR.at[k % 4], xs_s.at[s], xr_s.at[k % 4], 'x')
+        if k == 0:
+            @pl.loop(0, n)
             def _(j):
-                cols = pl.ds(al(j * CB, CB), CB)
-                dst[s, :, cols] = (mm(H[mb, pl.ds(row0, ROWS), :], W[s, 0, :, cols])
-                                   + mm(HC[mb, pl.ds(row0, ROWS), :], W[s, 1, :, cols]))
-        norm_ready(mb, 1)
-        half(ROWS, XS)
-        x_live[k] = rcopy(XS.at[s], XR.at[k % 4], xs_s.at[s], xr_s.at[k % 4], 'x')
-        x_live[k].start()
-        if k == 0:
+                half(j, 1)
+            x_live[k].start()
             w_start(1)
-        norm_ready(mb, 0)
-        half(0, XO)
+            norm_ready(mb, 0)
+
+            @pl.loop(0, n)
+            def _(j):
+                half(j, 0)
+        else:
+            norm_ready(mb, 0)
+
+            @pl.loop(0, 2 * n)
+            def _(i):
+                half(lax.rem(i, n), 1 - lax.div(i, n))
+
+                @pl.when(i == n - 1)
+                def _():
+                    x_live[k].start()
         w_start(k + 2)
 
     a_live = {}
@@ -174,24 +188,25 @@
         s, q = k % 2, k % 4
         x_live[k].wait_recv()
         if kind == 'q':
-            cos, sin = cos_ref[mb], sin_ref[mb]
-            for hh in range(QB // 128):
+
+            @pl.loop(0, QB // 128)
+            def _(hh):
                 def part(i):
-                    c0 = i * QB + hh * 128
-                    return XO[s, :, c0:c0 + 128] + XR[q, :, c0:c0 + 128]
+                    c = pl.ds(al(i * QB + hh * 128), 128)
+                    return XP[s, 0, :, c] + XR[q, :, c]
 
                 def rope(v):
-                    return (v * cos + pltpu.roll(v, 64, 1) * sin).astype(BF16)
+                    return (v * cos_ref[mb] + pltpu.roll(v, 64, 1) * sin_ref[mb]).astype(BF16)
                 qh, kh, vh = rope(part(0)), rope(part(1)), part(2).astype(BF16)
                 sc = lax.dot_general(qh, kh, (((1,), (1,)), ((), ())), preferred_element_type=F32) * (128 ** -0.5)
                 sc = jnp.where(mask_ref[mb] > 0.0, sc, NEG_BIG)
                 e = jnp.exp(sc - jnp.max(sc, axis=-1, keepdims=True))
                 p = (e / jnp.sum(e, axis=-1, keepdims=True)).astype(BF16)
-                ACT[mb, 0, :, b * QB + hh * 128:b * QB + hh * 128 + 128] = mm(p, vh).astype(BF16)
+                ACT[mb, 0, :, pl.ds(al(b * QB + hh * 128), 128)] = mm(p, vh).astype(BF16)
             cols = pl.ds(b * QB, QB)
         else:
-            g = XO[s, :, :GB] + XR[q, :, :GB]
-            u = XO[s, :, GB:] + XR[q, :, GB:]
+            g = XP[s, 0, :, :GB] + XR[q, :, :GB]
+            u = XP[s, 0, :, GB:] + XR[q, :, GB:]
             ACT[mb, 0, :, b * GB:(b + 1) * GB] = (jax.nn.silu(g) * u).astype(BF16)
             cols = pl.ds(b * GB, GB)
         c = rcopy(ACT.at[mb, 0, :, cols], ACT.at[mb, 1, :, cols], as_s.at[mb, b], ar_s.at[mb, b], 'x')
@@ -430,6 +445,9 @@
         row_wait()
         for xs in range(2):
             ac_live[mb, j, xs].wait()
+
+        @pl.loop(0, 2)
+        def _(xs):
             row_mm(mb, xs, a0, D_CHUNK, j == 0)
         row_done()
 
@@ -546,8 +564,7 @@
                 pltpu.VMEM((2, 256, FEAT), F32),
                 pltpu.VMEM((2, 512, FEAT), BF16),
                 pltpu.VMEM((2, 512, FEAT), BF16),
-                pltpu.VMEM((2, ROWS, SW), F32),
-                pltpu.VMEM((2, ROWS, SW), F32),
+                pltpu.VMEM((2, 2, ROWS, SW), F32),
                 pltpu.VMEM((4, ROWS, SW), F32),
                 pltpu.VMEM((2, 2, FEAT, SW), BF16),
                 pltpu.VMEM((2, HALF, FEAT), BF16),

time: 1230 us -> 1230 us (level)
  no operation moved by 1% of the time
where the time goes in v5:
time: 1230 us; the launch traced here: 1220 us
  Pallas kernels  1220 us (99%)
    pallas_call x1, Pallas kernels, device_fn(): pl.pallas_call(functools.partial(body, n_layers), out_shape=(jax.ShapeDty...  1220 us

profile of v5, /device:TPU:0, one launch (start us, length us, event | category | flops | bytes accessed | tf_op | source)
XLA Modules:
  0.0 1223.5 jit_solution(7114452632638839849)
XLA Ops:
  0.0 1.4 broadcast_in_dim.2.seg_ref
  1.4 1218.1 %shard_map.127 = (f32[2,64,5120]{2,1,0:T(8,128)}, bf16[2,3,10,1280,128]{4,3,2,1,0:T(8,128)(2,1)}, bf16[2,2,1280,3456]{3,2,1,0:T(8,128)(2,1)}) custom-call(bf16[2,64,5120]{2,1,0:T(8,128)(2,1)} %x_ref.1, s32[2,64,128]{2,1,0:T(8,128)} %broadcast_in_dim.2.seg_ref, f32[128,128]{1,0:T(8,128)} %constant.4.clone.ctab_ref, f32[128,128]{1,0:T(8,128)} %constant.5.clone.stab_ref, ...), custom_call_target="tpu_custom_call" | custom-call | tf_op jit(solution)/shard_map/pallas_call | solution.py:551
  1219.5 3.5 copy.15
